TPU v7x, 32 devices: a whole 2x2x4 slice. The times are simulated.
32 devices in a mesh: dp: 2 (over x), tp: 4 (over z), sp: 4 (over y, core).
Axes of the slice: x: 2, y: 2, z: 4, core: 2. Of those that a mesh axis runs over, the one named last changes fastest.
Arguments:
- x_in: bfloat16 [128, 2048], P('dp'), parts along dimension 0
- seq_lens: int32 [128], P('dp'), parts along dimension 0
- k_cache: bfloat16 [128, 512, 16, 128], P('dp', 'sp', 'tp'), parts along dimension 0
- v_cache: bfloat16 [128, 512, 16, 128], P('dp', 'sp', 'tp'), parts along dimension 0
- ln1_gain: float32 [2048], replicated
- w_qkv: bfloat16 [2048, 3, 16, 128], P(None, None, 'tp')
- w_out: bfloat16 [16, 128, 2048], P('tp')
- ln2_gain: float32 [2048], replicated
- w_up: bfloat16 [2048, 8192], P(None, 'tp')
- w_down: bfloat16 [8192, 2048], P('tp')
Outputs:
- output 1: bfloat16 [128, 2048], P('dp'), parts along dimension 0
- output 2: bfloat16 [128, 512, 16, 128], P('dp', 'sp', 'tp'), parts along dimension 0
- output 3: bfloat16 [128, 512, 16, 128], P('dp', 'sp', 'tp'), parts along dimension 0
There are 2 independent parts. A program takes and returns all parts, laid end to end along the dimension named above; an argument that names none is the same for every part.
All inputs are finite; a program needn't handle non-finite values.
Results may differ from a plain program's by a relative error of at most 0.00593826.
Values sent between devices are 32-bit elements.
A program may use at most 1 GiB of HBM per device.

v0:
```python
import jax
import jax.numpy as jnp
from jax import lax
from jax.sharding import PartitionSpec as P

LN_EPS = 1e-5


def layer_norm(x_f32, gain):
    mean = jnp.mean(x_f32, axis=-1, keepdims=True)
    centred = x_f32 - mean
    variance = jnp.mean(centred * centred, axis=-1, keepdims=True)
    return centred * lax.rsqrt(variance + LN_EPS) * gain


def solution(mesh):
    tp_size = mesh.shape["tp"]

    def local_layer(x_in, seq_lens, k_cache, v_cache, ln1_gain, w_qkv, w_out, ln2_gain, w_up, w_down):
        tok_dev = k_cache.shape[1]
        local_heads = k_cache.shape[2]
        head_dim = k_cache.shape[3]
        heads = local_heads * tp_size
        tp_index = lax.axis_index("tp")
        sp_index = lax.axis_index("sp")
        normed = layer_norm(x_in.astype(jnp.float32), ln1_gain).astype(jnp.bfloat16)
        qkv_proj = jnp.einsum("bd,dchk->bchk", normed, w_qkv, preferred_element_type=jnp.float32).astype(jnp.bfloat16)
        slot_pos = sp_index * tok_dev + jnp.arange(tok_dev)
        slot_hit = (slot_pos[None, :] == seq_lens[:, None])[:, :, None, None]
        k_next = jnp.where(slot_hit, qkv_proj[:, 1][:, None], k_cache)
        v_next = jnp.where(slot_hit, qkv_proj[:, 2][:, None], v_cache)
        head_ids = tp_index * local_heads + jnp.arange(local_heads)
        slopes = jnp.exp2(-8.0 * (head_ids + 1).astype(jnp.float32) / heads)
        scores = jnp.einsum("bhk,bthk->bht", qkv_proj[:, 0], k_next, preferred_element_type=jnp.float32) * head_dim ** -0.5
        distance = (seq_lens[:, None] - slot_pos[None, :]).astype(jnp.float32)
        scores = scores - slopes[None, :, None] * distance[:, None, :]
        is_valid = (slot_pos[None, :] <= seq_lens[:, None])[:, None, :]
        scores = jnp.where(is_valid, scores, -1e30)
        local_max = jnp.max(scores, axis=2)
        weights = jnp.where(is_valid, jnp.exp(scores - local_max[:, :, None]), 0.0)
        local_sum = jnp.sum(weights, axis=2)
        local_out = jnp.einsum("bht,bthk->bhk", weights.astype(jnp.bfloat16), v_next, preferred_element_type=jnp.float32)
        global_max = lax.pmax(local_max, "sp")
        rescale = jnp.exp(local_max - global_max)
        packed = jnp.concatenate([local_out * rescale[:, :, None], (local_sum * rescale)[:, :, None]], axis=2)
        packed = lax.psum(packed, "sp")
        attended = (packed[:, :, :head_dim] / packed[:, :, head_dim:]).astype(jnp.bfloat16)
        attn_part = jnp.einsum("bhk,hkd->bd", attended, w_out, preferred_element_type=jnp.float32)
        residual = x_in.astype(jnp.float32) + lax.psum(attn_part, "tp")
        normed_mid = layer_norm(residual, ln2_gain).astype(jnp.bfloat16)
        hidden = jax.nn.gelu(jnp.dot(normed_mid, w_up, preferred_element_type=jnp.float32), approximate=False).astype(jnp.bfloat16)
        down_part = jnp.dot(hidden, w_down, preferred_element_type=jnp.float32)
        x_out = (residual + lax.psum(down_part, "tp")).astype(jnp.bfloat16)
        return x_out, k_next, v_next

    cache_spec = P("dp", "sp", "tp", None)
    in_specs = (P("dp", None), P("dp"), cache_spec, cache_spec, P(None), P(None, None, "tp", None), P("tp", None, None), P(None), P(None, "tp"), P("tp", None))
    out_specs = (P("dp", None), cache_spec, cache_spec)
    return jax.shard_map(local_layer, mesh=mesh, in_specs=in_specs, out_specs=out_specs, check_vma=False)
```

profile of v0, /device:TPU:0, one launch (start us, length us, event | category | flops | bytes accessed | tf_op | source)
XLA Modules:
  0.0 187.9 jit_solution(8472762013960375183)
XLA Ops:
  7.2 0.0 copy-start
  7.2 0.0 all-reduce.4.cloned.1.call-start
  7.2 0.9 broadcast_compare_fusion.1
  8.1 0.7 subtract_convert_fusion
  8.8 0.0 copy-start.1
  8.9 1.2 convert_reduce_fusion
  10.1 1.5 fusion.11
  11.6 4.2 %fusion.6 = bf16[64,3,4,128]{3,0,2,1:T(8,128)(2,1)S(1)} fusion(bf16[2048,3,4,128]{3,2,1,0:T(4,128)(2,1)} %param.15, bf16[64,2048]{1,0:T(8,128)(2,1)} %param.10, f32[2048]{0:T(1024)} %param.14, f32[64]{0:T(128)S(1)} %add_rsqrt_fusion.1, f32[64]{0:T(128)S(1)} %broadcast_multiply_fusion.1), kind=kOutput, calls=%fused_computation.9 | convolution fusion | flops 403406848 | bytes 6758912 | tf_op jit(solution)/shard_map/bd,dchk->bchk/dot_general | solution.py:27
  15.8 0.1 copy.28
  15.9 0.1 copy.27
  15.9 0.0 copy-done.1
  15.9 13.7 %broadcast_select_fusion = (bf16[64,128,4,128]{3,2,1,0:T(4,128)(2,1)}, bf16[64,128,4,128]{3,2,1,0:T(4,128)(2,1)S(1)}) fusion(bf16[64,128,4,128]{3,2,1,0:T(4,128)(2,1)S(1)} %copy-done.1, pred[64,128]{1,0:T(8,128)(4,1)S(1)} %get-tuple-element.13, bf16[64,4,128]{2,1,0:T(4,128)(2,1)S(1)} %copy.28, bf16[64,128,4,128]{3,2,1,0:T(4,128)(2,1)} %param.12, ...), kind=kLoop, calls=%fused_computation.4 | loop fusion | flops 8388608 | bytes 33693696 | tf_op jit(solution)/shard_map/jit(_where)/select_n | solution.py:31
  29.6 0.0 copy-start.2
  29.6 3.4 %copy-done.2 = bf16[64,128,4,128]{3,2,1,0:T(4,128)(2,1)} copy-done((bf16[64,128,4,128]{3,2,1,0:T(4,128)(2,1)}, bf16[64,128,4,128]{3,2,1,0:T(4,128)(2,1)S(1)}, u32[]{:S(2)}) %copy-start.2) | copy-done | bytes 8388632
  33.0 4.4 %fusion.2 = f32[64,4,1,128]{3,2,1,0:T(1,128)S(1)} fusion(bf16[64,128,4,128]{3,2,1,0:T(4,128)(2,1)S(1)} %get-tuple-element.11, bf16[64,4,128,1]{2,0,1,3:T(8,128)(2,1)S(1)} %get-tuple-element.7), kind=kOutput, calls=%fused_computation.2 | convolution fusion | flops 8388608 | bytes 8585216 | tf_op jit(solution)/shard_map/bhk,bthk->bht/dot_general | solution.py:34
  37.4 0.0 copy-start.3
  37.4 0.0 copy-start.5
  37.4 0.2 fusion.109
  37.6 0.2 fusion.75
  37.8 8.4 %pmax.7 = f32[64,4]{0,1:T(4,128)S(1)} all-reduce(f32[64,4]{0,1:T(4,128)S(1)} %fusion.109), channel_id=1, replica_groups=mesh['dp'=2,'tp'=4,'sp'=4] {'sp'}, use_global_device_ids=true, to_apply=%region_3.4 | all-reduce | flops 256 | bytes 2048 | tf_op jit(solution)/shard_map/pmax | solution.py:43
  46.3 0.1 copy.29
  46.4 5.7 %fusion = f32[64,4,1,128]{3,2,1,0:T(1,128)S(1)} fusion(bf16[64,128,4,128]{3,2,1,0:T(4,128)(2,1)} %get-tuple-element.10, bf16[64,4,128,1]{2,0,1,3:T(8,128)(2,1)S(1)} %get-tuple-element.8), kind=kOutput, calls=%fused_computation | convolution fusion | flops 8388608 | bytes 8585216 | tf_op jit(solution)/shard_map/bht,bthk->bhk/dot_general | solution.py:42
  52.0 0.1 bitcast_multiply_fusion
  52.2 0.7 pad_maximum_fusion
  52.9 0.0 all-reduce.4.cloned.1.call-update
  52.9 0.0 all-reduce.6.cloned.1.call-start
  53.0 32.6 %all-reduce.4.cloned.1.call-done = f32[64,4,129]{2,0,1:T(8,128)} async-done(((f32[64,4,129]{2,0,1:T(8,128)}), f32[64,4,129]{2,0,1:T(8,128)}) %all-reduce.4.cloned.1.call-update) | async-done | bytes 132112 | tf_op jit(solution)/shard_map/psum | solution.py:46
  85.5 1.0 slice_reduce_fusion
  86.5 0.0 copy-done
  86.5 2.2 %convolution_bitcast_fusion = f32[64,2048]{1,0:T(8,128)} fusion(bf16[4,128,2048]{2,1,0:T(8,128)(2,1)S(1)} %copy-done, f32[64,4,129]{2,0,1:T(8,128)} %all-reduce.4.cloned.1.call-done, f32[64,4]{0,1:T(4,128)S(1)} %slice_reduce_fusion), kind=kOutput, calls=%fused_computation.8 | convolution fusion | flops 134283264 | bytes 2753536 | tf_op jit(solution)/shard_map/bhk,hkd->bd/dot_general | solution.py:48
  88.8 0.0 all-reduce.6.cloned.1.call-update
  88.8 0.0 all-reduce.8.cloned.1.call-start
  88.9 38.7 %all-reduce.6.cloned.1.call-done = f32[64,2048]{1,0:T(8,128)} async-done(((f32[64,2048]{1,0:T(8,128)}), f32[64,2048]{1,0:T(8,128)}) %all-reduce.6.cloned.1.call-update) | async-done | bytes 524304 | tf_op jit(solution)/shard_map/psum | solution.py:49
  127.6 0.0 copy-done.3
  127.6 1.2 fusion.78
  128.8 1.3 multiply_reduce_fusion
  130.1 0.0 copy-done.5
  130.1 0.0 copy-start.4
  130.1 10.9 %fusion.24 = f32[64,2048]{1,0:T(8,128)} fusion(bf16[2048,2048]{1,0:T(8,128)(2,1)} %param.19, bf16[2048,2048]{1,0:T(8,128)(2,1)} %param.18, f32[2048]{0:T(1024)S(1)} %copy-done.5, f32[64]{0:T(128)S(1)} %add_rsqrt_fusion, f32[64]{0:T(128)S(1)} %broadcast_multiply_fusion, f32[64,2048]{1,0:T(8,128)} %all-reduce.6.cloned.1.call-done, ...), kind=kOutput, calls=%fused_computation.40 | convolution fusion | flops 1083047936 | bytes 18096640 | tf_op jit(solution)/shard_map/dot_general | solution.py:52
  141.0 0.0 all-reduce.8.cloned.1.call-update
  141.0 38.5 %all-reduce.8.cloned.1.call-done = f32[64,2048]{1,0:T(8,128)} async-done(((f32[64,2048]{1,0:T(8,128)}), f32[64,2048]{1,0:T(8,128)}) %all-reduce.8.cloned.1.call-update) | async-done | bytes 524304 | tf_op jit(solution)/shard_map/psum | solution.py:53
  179.5 0.0 copy-done.4
  179.5 1.8 add_convert_fusion
  (8 shorter events, 0.1 us)
Async XLA Ops:
  7.2 79.4 %copy-start = (bf16[4,128,2048]{2,1,0:T(8,128)(2,1)S(1)}, bf16[4,128,2048]{2,1,0:T(8,128)(2,1)}, u32[]{:S(2)}) copy-start(bf16[4,128,2048]{2,1,0:T(8,128)(2,1)} %param.16) | copy-start | bytes 6291460
  7.2 78.3 %all-reduce.4.cloned.1.call-start = ((), (), s32[]{:S(2)}) async-start(), calls=%async_computation | async-start | bytes 524288 | tf_op jit(solution)/shard_map/psum | solution.py:46
  8.8 7.1 %copy-start.1 = (bf16[64,128,4,128]{3,2,1,0:T(4,128)(2,1)S(1)}, bf16[64,128,4,128]{3,2,1,0:T(4,128)(2,1)}, u32[]{:S(2)}) copy-start(bf16[64,128,4,128]{3,2,1,0:T(4,128)(2,1)} %param.13) | copy-start | bytes 25165828
  29.6 3.4 %copy-start.2 = (bf16[64,128,4,128]{3,2,1,0:T(4,128)(2,1)}, bf16[64,128,4,128]{3,2,1,0:T(4,128)(2,1)S(1)}, u32[]{:S(2)}) copy-start(bf16[64,128,4,128]{3,2,1,0:T(4,128)(2,1)S(1)} %get-tuple-element.11) | copy-start | bytes 25165828
  37.4 90.2 %copy-start.3 = (bf16[64,2048]{1,0:T(8,128)(2,1)S(1)}, bf16[64,2048]{1,0:T(8,128)(2,1)}, u32[]{:S(2)}) copy-start(bf16[64,2048]{1,0:T(8,128)(2,1)} %param.10) | copy-start | bytes 786436
  37.4 92.7 %copy-start.5 = (f32[2048]{0:T(1024)S(1)}, f32[2048]{0:T(1024)}, u32[]{:S(2)}) copy-start(f32[2048]{0:T(1024)} %param.17) | copy-start | bytes 24580
  52.9 74.7 %all-reduce.6.cloned.1.call-start = ((), (), s32[]{:S(2)}) async-start(), calls=%async_computation.1 | async-start | bytes 1048576 | tf_op jit(solution)/shard_map/psum | solution.py:49
  88.8 90.7 %all-reduce.8.cloned.1.call-start = ((), (), s32[]{:S(2)}) async-start(), calls=%async_computation.2 | async-start | bytes 1048576 | tf_op jit(solution)/shard_map/psum | solution.py:53
  130.1 49.5 %copy-start.4 = (f32[64,2048]{1,0:T(8,128)S(1)}, f32[64,2048]{1,0:T(8,128)}, u32[]{:S(2)}) copy-start(f32[64,2048]{1,0:T(8,128)} %all-reduce.6.cloned.1.call-done) | copy-start | bytes 1572868
Sparse Core Ops, SparseCore 0:
  53.0 32.4 all-reduce.3
  88.9 38.5 all-reduce.5
  141.2 38.3 all-reduce.7
where the time goes:
time: 188 us
  waiting for transfers between devices  110 us (59%)
  matrix products  27.4 us (15%)
  other arithmetic  23.5 us (12%)
  between operations  13.9 us (7%)
  blocking collectives  8.43 us (4%)
  local copies, waits for them, and re-layouts  4.67 us (2%)
    psum x1, waiting for transfers between devices, local_layer(): residual = x_in.astype(jnp.float32) + lax.psum(attn_part, 'tp')  38.7 us
    psum x1, waiting for transfers between devices, local_layer(): x_out = (residual + lax.psum(down_part, 'tp')).astype(jnp.bfloat16)  38.5 us
    psum x1, waiting for transfers between devices, local_layer(): packed = lax.psum(packed, 'sp')  32.6 us
    select_n x1, other arithmetic, local_layer(): v_next = jnp.where(slot_hit, qkv_proj[:, 2][:, None], v_cache)  13.7 us
    dot_general x1, matrix products, local_layer(): down_part = jnp.dot(hidden, w_down, preferred_element_type=jnp.float32)  10.9 us
    pmax x1, blocking collectives, local_layer(): global_max = lax.pmax(local_max, 'sp')  8.43 us
    dot_general x1, matrix products, local_layer(): jnp.einsum('bht,bthk->bhk', weights.astype(jnp.bfloat16), v_next, preferr...  5.65 us
    dot_general x1, matrix products, local_layer(): jnp.einsum('bhk,bthk->bht', qkv_proj[:, 0], k_next, preferred_element_typ...  4.41 us
  transfers between devices with their start and end apart: 3, of which 3 were waited for; matrix products, arithmetic and copies ran while one was open for 0% of the time, Pallas kernels for 0%

commit v1 on v0

--- a/solution.py
+++ b/solution.py
@@ -1,9 +1,14 @@
+import functools
+
 import jax
 import jax.numpy as jnp
 from jax import lax
+from jax.experimental import pallas as pl
+from jax.experimental.pallas import tpu as pltpu
 from jax.sharding import PartitionSpec as P
 
 LN_EPS = 1e-5
+MESH = pl.DeviceIdType.MESH
 
 
 def layer_norm(x_f32, gain):
@@ -13,8 +18,184 @@
     return centred * lax.rsqrt(variance + LN_EPS) * gain
 
 
+def gelu(x):
+    return 0.5 * x * (1.0 + lax.erf(x * (0.5 ** 0.5)))
+
+
+def tail_kernel(tp, sp, heads, hd, pay_ref, x_ref, gain_ref, wo_hbm, wu_hbm, wd_hbm, out_ref,
+                wo, wu, wd, got_pay, part, got_part, r_all, h_mid, hidden, down, got_down, x_all,
+                wo_sem, wu_sem, wd_sem, s1, r1, s2, r2, s3, r3, s4, r4, s5z, s5y, s5c, r5):
+    my_tp = lax.axis_index("tp")
+    my_sp = lax.axis_index("sp")
+    rows = x_ref.shape[0] // sp
+    cols = x_ref.shape[1] // tp
+
+    barrier = pltpu.get_barrier_semaphore()
+    for off in range(1, sp):
+        pl.semaphore_signal(barrier, inc=1, device_id={"sp": lax.rem(my_sp + off, sp)}, device_id_type=MESH)
+    for off in range(1, tp):
+        pl.semaphore_signal(barrier, inc=1, device_id={"tp": lax.rem(my_tp + off, tp)}, device_id_type=MESH)
+
+    loads = {}
+    for name, src, dst, sem in (("o", wo_hbm, wo, wo_sem), ("u", wu_hbm, wu, wu_sem), ("d", wd_hbm, wd, wd_sem)):
+        for j in range(tp):
+            copy = pltpu.make_async_copy(src.at[:, pl.ds(j * cols, cols)], dst.at[j], sem.at[j])
+            copy.start()
+            loads[name, j] = copy
+
+    pl.semaphore_wait(barrier, sp + tp - 2)
+
+    sends = []
+    for off in range(1, sp):
+        peer = lax.rem(my_sp + off, sp)
+        copy = pltpu.make_async_remote_copy(
+            pay_ref.at[pl.ds(pl.multiple_of(peer * rows, rows), rows)], got_pay.at[my_sp],
+            s1.at[off], r1.at[my_sp], device_id={"sp": peer}, device_id_type=MESH)
+        copy.start()
+        sends.append(copy)
+
+    def arrived(dst, sem):
+        pltpu.make_async_copy(dst, dst, sem).wait()
+
+    blocks = [pay_ref[pl.ds(pl.multiple_of(my_sp * rows, rows), rows), :]]
+    for off in range(1, sp):
+        peer = lax.rem(my_sp + off, sp)
+        arrived(got_pay.at[peer], r1.at[peer])
+        blocks.append(got_pay[peer])
+    width = heads * hd
+    stats = [b[:, width:] for b in blocks]
+    top = functools.reduce(jnp.maximum, stats)
+    scale = [jnp.exp(s - top) for s in stats]
+    attended = []
+    for h in range(heads):
+        num = sum(c[:, h:h + 1] * b[:, h * hd:(h + 1) * hd] for c, b in zip(scale, blocks))
+        den = sum(c[:, h:h + 1] * s[:, heads + h:heads + h + 1] for c, s in zip(scale, stats))
+        attended.append(num / den)
+    attended = jnp.concatenate(attended, axis=1).astype(jnp.bfloat16)
+
+    for j in range(tp):
+        loads["o", j].wait()
+    for off in range(1, tp):
+        peer = lax.rem(my_tp + off, tp)
+        part[peer] = jnp.dot(attended, wo[peer], preferred_element_type=jnp.float32)
+        copy = pltpu.make_async_remote_copy(part.at[peer], got_part.at[my_tp], s2.at[off], r2.at[my_tp],
+                                            device_id={"tp": peer}, device_id_type=MESH)
+        copy.start()
+        sends.append(copy)
+    mine = jnp.dot(attended, wo[my_tp], preferred_element_type=jnp.float32)
+    row0 = pl.multiple_of(my_sp * rows, rows)
+    mine += x_ref[pl.ds(row0, rows), pl.ds(pl.multiple_of(my_tp * cols, cols), cols)].astype(jnp.float32)
+    for off in range(1, tp):
+        peer = lax.rem(my_tp + off, tp)
+        arrived(got_part.at[peer], r2.at[peer])
+        mine += got_part[peer]
+    r_all[my_tp] = mine
+    for off in range(1, tp):
+        peer = lax.rem(my_tp + off, tp)
+        copy = pltpu.make_async_remote_copy(r_all.at[my_tp], r_all.at[my_tp], s3.at[off], r3.at[my_tp],
+                                            device_id={"tp": peer}, device_id_type=MESH)
+        copy.start()
+        sends.append(copy)
+    for off in range(1, tp):
+        peer = lax.rem(my_tp + off, tp)
+        arrived(r_all.at[peer], r3.at[peer])
+
+    r = jnp.concatenate([r_all[j] for j in range(tp)], axis=1)
+    h_mid[...] = layer_norm(r, gain_ref[...]).astype(jnp.bfloat16)
+
+    for j in range(tp):
+        loads["u", j].wait()
+        up = jnp.dot(h_mid[...], wu[j], preferred_element_type=jnp.float32)
+        hidden[:, j * cols:(j + 1) * cols] = gelu(up).astype(jnp.bfloat16)
+
+    for j in range(tp):
+        loads["d", j].wait()
+    for off in range(1, tp):
+        peer = lax.rem(my_tp + off, tp)
+        down[peer] = jnp.dot(hidden[...], wd[peer], preferred_element_type=jnp.float32)
+        copy = pltpu.make_async_remote_copy(down.at[peer], got_down.at[my_tp], s4.at[off], r4.at[my_tp],
+                                            device_id={"tp": peer}, device_id_type=MESH)
+        copy.start()
+        sends.append(copy)
+    mine = r_all[my_tp] + jnp.dot(hidden[...], wd[my_tp], preferred_element_type=jnp.float32)
+    for off in range(1, tp):
+        peer = lax.rem(my_tp + off, tp)
+        arrived(got_down.at[peer], r4.at[peer])
+        mine += got_down[peer]
+    x_all[my_sp, my_tp] = mine.astype(jnp.bfloat16).astype(jnp.float32)
+
+    side = lax.rem(my_sp + 2, sp)
+    twin = my_sp + 1 - 2 * lax.rem(my_sp, 2)
+    side_twin = lax.rem(twin + 2, sp)
+
+    def pass_on(s, t, send_sem, slot, to):
+        copy = pltpu.make_async_remote_copy(x_all.at[s, t], x_all.at[s, t], send_sem.at[slot], r5.at[s, t],
+                                            device_id=to, device_id_type=MESH)
+        copy.start()
+        sends.append(copy)
+
+    for off in range(1, tp):
+        pass_on(my_sp, my_tp, s5z, off, {"tp": lax.rem(my_tp + off, tp)})
+    pass_on(my_sp, my_tp, s5y, 0, {"sp": side})
+    pass_on(my_sp, my_tp, s5c, 0, {"sp": twin})
+    for off in range(1, tp):
+        peer = lax.rem(my_tp + off, tp)
+        arrived(x_all.at[my_sp, peer], r5.at[my_sp, peer])
+        pass_on(my_sp, peer, s5y, off, {"sp": side})
+        pass_on(my_sp, peer, s5c, off, {"sp": twin})
+    for off in range(tp):
+        peer = lax.rem(my_tp + off, tp)
+        arrived(x_all.at[side, peer], r5.at[side, peer])
+        pass_on(side, peer, s5c, tp + off, {"sp": twin})
+    for who in (twin, side_twin):
+        for off in range(tp):
+            peer = lax.rem(my_tp + off, tp)
+            arrived(x_all.at[who, peer], r5.at[who, peer])
+    for s in range(sp):
+        for t in range(tp):
+            out_ref[s * rows:(s + 1) * rows, t * cols:(t + 1) * cols] = x_all[s, t].astype(jnp.bfloat16)
+    for copy in sends:
+        copy.wait_send()
+
+
+def tail(tp, sp, heads, hd, pay, x_in, gain, w_out, w_up, w_down):
+    batch, d = x_in.shape
+    rows, cols = batch // sp, d // tp
+    ff = w_up.shape[1]
+    width = heads * hd
+    vmem = pl.BlockSpec(memory_space=pltpu.VMEM)
+    hbm = pl.BlockSpec(memory_space=pl.ANY)
+    dma = pltpu.SemaphoreType.DMA
+    return pl.pallas_call(
+        functools.partial(tail_kernel, tp, sp, heads, hd),
+        out_shape=jax.ShapeDtypeStruct((batch, d), jnp.bfloat16),
+        in_specs=[vmem, vmem, vmem, hbm, hbm, hbm],
+        out_specs=vmem,
+        scratch_shapes=[
+            pltpu.VMEM((tp, width, cols), jnp.bfloat16),
+            pltpu.VMEM((tp, d, ff // tp), jnp.bfloat16),
+            pltpu.VMEM((tp, ff, cols), jnp.bfloat16),
+            pltpu.VMEM((sp, rows, pay.shape[1]), jnp.float32),
+            pltpu.VMEM((tp, rows, cols), jnp.float32),
+            pltpu.VMEM((tp, rows, cols), jnp.float32),
+            pltpu.VMEM((tp, rows, cols), jnp.float32),
+            pltpu.VMEM((rows, d), jnp.bfloat16),
+            pltpu.VMEM((rows, ff), jnp.bfloat16),
+            pltpu.VMEM((tp, rows, cols), jnp.float32),
+            pltpu.VMEM((tp, rows, cols), jnp.float32),
+            pltpu.VMEM((sp, tp, rows, cols), jnp.float32),
+            dma((tp,)), dma((tp,)), dma((tp,)),
+            dma((sp,)), dma((sp,)), dma((tp,)), dma((tp,)), dma((tp,)), dma((tp,)), dma((tp,)), dma((tp,)),
+            dma((tp,)), dma((tp,)), dma((2 * tp,)), dma((sp, tp)),
+        ],
+        compiler_params=pltpu.CompilerParams(collective_id=0, has_side_effects=True, vmem_limit_bytes=32 * 2 ** 20),
+        name="tail",
+    )(pay, x_in, gain[None, :], w_out.reshape(width, d), w_up, w_down)
+
+
 def solution(mesh):
     tp_size = mesh.shape["tp"]
+    sp_size = mesh.shape["sp"]
 
     def local_layer(x_in, seq_lens, k_cache, v_cache, ln1_gain, w_qkv, w_out, ln2_gain, w_up, w_down):
         tok_dev = k_cache.shape[1]
@@ -40,17 +221,10 @@
         weights = jnp.where(is_valid, jnp.exp(scores - local_max[:, :, None]), 0.0)
         local_sum = jnp.sum(weights, axis=2)
         local_out = jnp.einsum("bht,bthk->bhk", weights.astype(jnp.bfloat16), v_next, preferred_element_type=jnp.float32)
-        global_max = lax.pmax(local_max, "sp")
-        rescale = jnp.exp(local_max - global_max)
-        packed = jnp.concatenate([local_out * rescale[:, :, None], (local_sum * rescale)[:, :, None]], axis=2)
-        packed = lax.psum(packed, "sp")
-        attended = (packed[:, :, :head_dim] / packed[:, :, head_dim:]).astype(jnp.bfloat16)
-        attn_part = jnp.einsum("bhk,hkd->bd", attended, w_out, preferred_element_type=jnp.float32)
-        residual = x_in.astype(jnp.float32) + lax.psum(attn_part, "tp")
-        normed_mid = layer_norm(residual, ln2_gain).astype(jnp.bfloat16)
-        hidden = jax.nn.gelu(jnp.dot(normed_mid, w_up, preferred_element_type=jnp.float32), approximate=False).astype(jnp.bfloat16)
-        down_part = jnp.dot(hidden, w_down, preferred_element_type=jnp.float32)
-        x_out = (residual + lax.psum(down_part, "tp")).astype(jnp.bfloat16)
+        batch = x_in.shape[0]
+        filler = jnp.zeros((batch, 128 - 2 * local_heads), jnp.float32)
+        pay = jnp.concatenate([local_out.reshape(batch, -1), local_max, local_sum, filler], axis=1)
+        x_out = tail(tp_size, sp_size, local_heads, head_dim, pay, x_in, ln2_gain, w_out, w_up, w_down)
         return x_out, k_next, v_next
 
     cache_spec = P("dp", "sp", "tp", None)

time: 188 us -> 78 us (0.41)
  waiting for transfers between devices: 110 us -> 0 us
  Pallas kernels: 0 us -> 33.1 us
  matrix products: 27.4 us -> 14.2 us
  between operations: 13.9 us -> 0.78 us
  blocking collectives: 8.43 us -> 0 us
  local copies, waits for them, and re-layouts: 4.67 us -> 11.3 us
  other arithmetic: 23.5 us -> 18.3 us
    psum x3 -> x0, waiting for transfers between devices: 110 us -> none  [the longest x1 38.7 us: local_layer(): residual = x_in.astype(jnp.float32) + lax.psum(attn_part, 'tp')]
    pallas_call x0 -> x1, Pallas kernels: none -> 33.1 us  [tail(): pl.pallas_call(functools.partial(tail_kernel, tp, sp, heads, hd), out_sha...]
    dot_general x2 -> x0, matrix products: 13.2 us -> none  [the longest x1 10.9 us: local_layer(): down_part = jnp.dot(hidden, w_down, preferred_element_type=jnp.float32)]
    pmax x1 -> x0, blocking collectives: 8.43 us -> none  [local_layer(): global_max = lax.pmax(local_max, 'sp')]
    unnamed x12 -> x16, local copies, waits for them, and re-layouts: 3.42 us -> 10.9 us
  transfers between devices with their start and end apart: 3 -> 0, of which waited for: 3 -> 0; matrix products, arithmetic and copies ran while one was open for 0% -> 0% of each run, Pallas kernels for 0% -> 0%
where the time goes in v1:
time: 78 us; the launch traced here: 77.7 us
  Pallas kernels  33.1 us (42%)
  other arithmetic  18.3 us (23%)
  matrix products  14.2 us (18%)
  local copies, waits for them, and re-layouts  11.3 us (14%)
  between operations  0.78 us (1%)
    pallas_call x1, Pallas kernels, tail(): pl.pallas_call(functools.partial(tail_kernel, tp, sp, heads, hd), out_sha...  33.1 us
    select_n x1, other arithmetic, local_layer(): v_next = jnp.where(slot_hit, qkv_proj[:, 2][:, None], v_cache)  13.7 us
    unnamed x16, local copies, waits for them, and re-layouts  10.9 us
    dot_general x1, matrix products, local_layer(): jnp.einsum('bht,bthk->bhk', weights.astype(jnp.bfloat16), v_next, preferr...  5.66 us
    dot_general x1, matrix products, local_layer(): jnp.einsum('bhk,bthk->bht', qkv_proj[:, 0], k_next, preferred_element_typ...  4.41 us
    dot_general x1, matrix products, local_layer(): jnp.einsum('bd,dchk->bchk', normed, w_qkv, preferred_element_type=jnp.flo...  4.16 us

profile of v1, /device:TPU:0, one launch (start us, length us, event | category | flops | bytes accessed | tf_op | source)
XLA Modules:
  0.0 77.7 jit_solution(3449551748783408477)
XLA Ops:
  0.6 0.0 copy-start.5
  0.7 1.2 %convert_reduce_fusion = f32[64]{0:T(128)S(1)} fusion(bf16[64,2048]{1,0:T(8,128)(2,1)} %x_ref.1), kind=kLoop, calls=%fused_computation.10 | loop fusion | flops 262080 | bytes 262400 | tf_op jit(solution)/shard_map/reduce_sum | solution.py:15
  1.9 1.5 %fusion.11 = f32[64]{0:T(128)S(1)} fusion(bf16[64,2048]{1,0:T(8,128)(2,1)} %x_ref.1, f32[64]{0:T(128)S(1)} %broadcast_multiply_fusion), kind=kLoop, calls=%fused_computation.13 | loop fusion | flops 524224 | bytes 262656 | tf_op jit(solution)/shard_map/reduce_sum | solution.py:17
  3.4 0.1 pad.3.clone
  3.5 0.7 broadcast_compare_fusion.1
  4.2 0.7 subtract_convert_fusion
  5.0 4.2 %fusion.6 = bf16[64,3,4,128]{3,0,2,1:T(8,128)(2,1)S(1)} fusion(bf16[2048,3,4,128]{3,2,1,0:T(4,128)(2,1)} %param.15, bf16[64,2048]{1,0:T(8,128)(2,1)} %x_ref.1, f32[2048]{0:T(1024)} %param.14, f32[64]{0:T(128)S(1)} %add_rsqrt_fusion, f32[64]{0:T(128)S(1)} %broadcast_multiply_fusion), kind=kOutput, calls=%fused_computation.8 | convolution fusion | flops 403406848 | bytes 6758912 | tf_op jit(solution)/shard_map/bd,dchk->bchk/dot_general | solution.py:208
  9.2 0.1 copy.18
  9.2 0.1 copy.17
  9.3 0.0 copy-done.5
  9.3 13.7 %broadcast_select_fusion = (bf16[64,128,4,128]{3,2,1,0:T(4,128)(2,1)}, bf16[64,128,4,128]{3,2,1,0:T(4,128)(2,1)S(1)}) fusion(bf16[64,128,4,128]{3,2,1,0:T(4,128)(2,1)S(1)} %copy-done.5, pred[64,128]{1,0:T(8,128)(4,1)S(1)} %get-tuple-element.11, bf16[64,4,128]{2,1,0:T(4,128)(2,1)S(1)} %copy.18, bf16[64,128,4,128]{3,2,1,0:T(4,128)(2,1)} %param.12, ...), kind=kLoop, calls=%fused_computation.4 | loop fusion | flops 8388608 | bytes 33693696 | tf_op jit(solution)/shard_map/jit(_where)/select_n | solution.py:212
  23.0 0.0 copy-start.6
  23.0 3.4 %copy-done.6 = bf16[64,128,4,128]{3,2,1,0:T(4,128)(2,1)} copy-done((bf16[64,128,4,128]{3,2,1,0:T(4,128)(2,1)}, bf16[64,128,4,128]{3,2,1,0:T(4,128)(2,1)S(1)}, u32[]{:S(2)}) %copy-start.6) | copy-done | bytes 8388632
  26.3 0.0 copy-start.2
  26.4 0.0 copy-start.3
  26.4 0.0 copy-start.4
  26.4 4.4 %fusion.2 = f32[64,4,1,128]{3,2,1,0:T(1,128)S(1)} fusion(bf16[64,128,4,128]{3,2,1,0:T(4,128)(2,1)S(1)} %get-tuple-element.16, bf16[64,4,128,1]{2,0,1,3:T(8,128)(2,1)S(1)} %get-tuple-element.5), kind=kOutput, calls=%fused_computation.2 | convolution fusion | flops 8388608 | bytes 8585216 | tf_op jit(solution)/shard_map/bhk,bthk->bht/dot_general | solution.py:215
  30.8 0.2 fusion.26
  31.0 0.2 fusion.25
  31.2 0.1 copy.19
  31.3 0.1 copy.20
  31.4 5.7 %fusion = f32[64,4,1,128]{3,2,1,0:T(1,128)S(1)} fusion(bf16[64,128,4,128]{3,2,1,0:T(4,128)(2,1)} %get-tuple-element.17, bf16[64,4,128,1]{2,0,1,3:T(8,128)(2,1)S(1)} %get-tuple-element.6), kind=kOutput, calls=%fused_computation | convolution fusion | flops 8388608 | bytes 8585216 | tf_op jit(solution)/shard_map/bht,bthk->bhk/dot_general | solution.py:223
  37.1 0.1 maximum_maximum_fusion.pay_ref
  37.1 0.0 copy-done.2
  37.1 0.0 copy-done.3
  37.1 0.0 copy-done.4
  37.2 0.0 copy-start
  37.2 3.4 %copy-done = bf16[2048,2048]{1,0:T(8,128)(2,1)S(1)} copy-done((bf16[2048,2048]{1,0:T(8,128)(2,1)S(1)}, bf16[2048,2048]{1,0:T(8,128)(2,1)}, u32[]{:S(2)}) %copy-start) | copy-done | bytes 8388632
  40.5 0.0 copy-start.1
  40.5 3.4 %copy-done.1 = bf16[2048,2048]{1,0:T(8,128)(2,1)S(1)} copy-done((bf16[2048,2048]{1,0:T(8,128)(2,1)S(1)}, bf16[2048,2048]{1,0:T(8,128)(2,1)}, u32[]{:S(2)}) %copy-start.1) | copy-done | bytes 8388632
  43.9 33.1 %tail.1 = bf16[64,2048]{1,0:T(8,128)(2,1)S(1)} custom-call(f32[64,640]{1,0:T(8,128)S(1)} %maximum_maximum_fusion.pay_ref, bf16[64,2048]{1,0:T(8,128)(2,1)S(1)} %copy-done.2, f32[1,2048]{1,0:T(1,128)S(1)} %bitcast.35, bf16[512,2048]{1,0:T(8,128)(2,1)S(1)} %bitcast.34, bf16[2048,2048]{1,0:T(8,128)(2,1)S(1)} %copy-done, bf16[2048,2048]{1,0:T(8,128)(2,1)S(1)} %copy-done.1), custom_call_target="tpu_custom_call" | custom-call | tf_op jit(solution)/shard_map/tail/pallas_call | solution.py:169
  77.0 0.7 copy.51
  (7 shorter events, 0.1 us)
Async XLA Ops:
  0.6 8.7 %copy-start.5 = (bf16[64,128,4,128]{3,2,1,0:T(4,128)(2,1)S(1)}, bf16[64,128,4,128]{3,2,1,0:T(4,128)(2,1)}, u32[]{:S(2)}) copy-start(bf16[64,128,4,128]{3,2,1,0:T(4,128)(2,1)} %param.13) | copy-start | bytes 25165828
  23.0 3.4 %copy-start.6 = (bf16[64,128,4,128]{3,2,1,0:T(4,128)(2,1)}, bf16[64,128,4,128]{3,2,1,0:T(4,128)(2,1)S(1)}, u32[]{:S(2)}) copy-start(bf16[64,128,4,128]{3,2,1,0:T(4,128)(2,1)S(1)} %get-tuple-element.16) | copy-start | bytes 25165828
  26.3 10.8 %copy-start.2 = (bf16[64,2048]{1,0:T(8,128)(2,1)S(1)}, bf16[64,2048]{1,0:T(8,128)(2,1)}, u32[]{:S(2)}) copy-start(bf16[64,2048]{1,0:T(8,128)(2,1)} %x_ref.1) | copy-start | bytes 786436
  26.4 10.8 %copy-start.3 = (bf16[4,128,2048]{2,1,0:T(8,128)(2,1)S(1)}, bf16[4,128,2048]{2,1,0:T(8,128)(2,1)}, u32[]{:S(2)}) copy-start(bf16[4,128,2048]{2,1,0:T(8,128)(2,1)} %param.16) | copy-start | bytes 6291460
  26.4 10.8 %copy-start.4 = (f32[2048]{0:T(1024)S(1)}, f32[2048]{0:T(1024)}, u32[]{:S(2)}) copy-start(f32[2048]{0:T(1024)} %param.17) | copy-start | bytes 24580
  37.2 3.4 %copy-start = (bf16[2048,2048]{1,0:T(8,128)(2,1)S(1)}, bf16[2048,2048]{1,0:T(8,128)(2,1)}, u32[]{:S(2)}) copy-start(bf16[2048,2048]{1,0:T(8,128)(2,1)} %wu_hbm.1) | copy-start | bytes 25165828
  40.5 3.4 %copy-start.1 = (bf16[2048,2048]{1,0:T(8,128)(2,1)S(1)}, bf16[2048,2048]{1,0:T(8,128)(2,1)}, u32[]{:S(2)}) copy-start(bf16[2048,2048]{1,0:T(8,128)(2,1)} %wd_hbm.1) | copy-start | bytes 25165828

commit v2 on v1

--- a/solution.py
+++ b/solution.py
@@ -23,7 +23,7 @@
 
 
 def tail_kernel(tp, sp, heads, hd, pay_ref, x_ref, gain_ref, wo_hbm, wu_hbm, wd_hbm, out_ref,
-                wo, wu, wd, got_pay, part, got_part, r_all, h_mid, hidden, down, got_down, x_all,
+                wo, wu, wd, got_pay, att, part, got_part, r_all, h_mid, hidden, down, got_down, x_all,
                 wo_sem, wu_sem, wd_sem, s1, r1, s2, r2, s3, r3, s4, r4, s5z, s5y, s5c, r5):
     my_tp = lax.axis_index("tp")
     my_sp = lax.axis_index("sp")
@@ -49,7 +49,7 @@
     for off in range(1, sp):
         peer = lax.rem(my_sp + off, sp)
         copy = pltpu.make_async_remote_copy(
-            pay_ref.at[pl.ds(pl.multiple_of(peer * rows, rows), rows)], got_pay.at[my_sp],
+            pay_ref.at[peer], got_pay.at[my_sp],
             s1.at[off], r1.at[my_sp], device_id={"sp": peer}, device_id_type=MESH)
         copy.start()
         sends.append(copy)
@@ -57,21 +57,19 @@
     def arrived(dst, sem):
         pltpu.make_async_copy(dst, dst, sem).wait()
 
-    blocks = [pay_ref[pl.ds(pl.multiple_of(my_sp * rows, rows), rows), :]]
+    pairs = rows * heads
+    blocks = [pay_ref[my_sp]]
     for off in range(1, sp):
         peer = lax.rem(my_sp + off, sp)
         arrived(got_pay.at[peer], r1.at[peer])
         blocks.append(got_pay[peer])
-    width = heads * hd
-    stats = [b[:, width:] for b in blocks]
-    top = functools.reduce(jnp.maximum, stats)
-    scale = [jnp.exp(s - top) for s in stats]
-    attended = []
-    for h in range(heads):
-        num = sum(c[:, h:h + 1] * b[:, h * hd:(h + 1) * hd] for c, b in zip(scale, blocks))
-        den = sum(c[:, h:h + 1] * s[:, heads + h:heads + h + 1] for c, s in zip(scale, stats))
-        attended.append(num / den)
-    attended = jnp.concatenate(attended, axis=1).astype(jnp.bfloat16)
+    top = functools.reduce(jnp.maximum, [b[pairs:pairs + 1] for b in blocks])
+    scale = [jnp.exp(b[pairs:pairs + 1] - top) for b in blocks]
+    den = sum(c * b[pairs + 1:pairs + 2] for c, b in zip(scale, blocks))
+    coef = jnp.concatenate(scale + [den] * (8 - sp), axis=0).T
+    coef = jnp.where(lax.rem(my_sp, 2) == 0, coef[:pairs], coef[pairs:])
+    att[...] = sum(coef[:, i:i + 1] * b[:pairs] for i, b in enumerate(blocks)) / coef[:, sp:sp + 1]
+    attended = jnp.concatenate([att[pl.ds(h, rows, stride=heads), :] for h in range(heads)], axis=1).astype(jnp.bfloat16)
 
     for j in range(tp):
         loads["o", j].wait()
@@ -175,7 +173,8 @@
             pltpu.VMEM((tp, width, cols), jnp.bfloat16),
             pltpu.VMEM((tp, d, ff // tp), jnp.bfloat16),
             pltpu.VMEM((tp, ff, cols), jnp.bfloat16),
-            pltpu.VMEM((sp, rows, pay.shape[1]), jnp.float32),
+            pltpu.VMEM(pay.shape, jnp.float32),
+            pltpu.VMEM((rows * heads, hd), jnp.float32),
             pltpu.VMEM((tp, rows, cols), jnp.float32),
             pltpu.VMEM((tp, rows, cols), jnp.float32),
             pltpu.VMEM((tp, rows, cols), jnp.float32),
@@ -188,9 +187,123 @@
             dma((sp,)), dma((sp,)), dma((tp,)), dma((tp,)), dma((tp,)), dma((tp,)), dma((tp,)), dma((tp,)),
             dma((tp,)), dma((tp,)), dma((2 * tp,)), dma((sp, tp)),
         ],
-        compiler_params=pltpu.CompilerParams(collective_id=0, has_side_effects=True, vmem_limit_bytes=32 * 2 ** 20),
+        compiler_params=pltpu.CompilerParams(collective_id=0, has_side_effects=True, vmem_limit_bytes=60 * 2 ** 20),
         name="tail",
     )(pay, x_in, gain[None, :], w_out.reshape(width, d), w_up, w_down)
+
+
+def attend_kernel(lens_ref, qkv_ref, k_hbm, v_hbm, pay_ref, kn_hbm, vn_hbm,
+                  kbuf, vbuf, rep_k, rep_v, p_t, k_in, v_in, k_out, v_out, *, heads, all_heads, sp, chunks):
+    batch, pairs, hd = kbuf.shape
+    slots = pairs // heads
+    per = batch // chunks
+    base = lax.axis_index("sp") * slots
+
+    def moves(src, dst, sem, c):
+        part = pl.ds(c * per, per)
+        return pltpu.make_async_copy(src.at[part], dst.at[part], sem.at[c])
+
+    for c in range(chunks):
+        moves(k_hbm, kbuf, k_in, c).start()
+    for c in range(chunks):
+        moves(v_hbm, vbuf, v_in, c).start()
+
+    low = lax.broadcasted_iota(jnp.int32, (1, 8, hd), 1) < heads
+    for rep, i in ((rep_k, 1), (rep_v, 2)):
+        new = qkv_ref[i].reshape(batch // 2, 8, hd)
+        turned = pltpu.roll(new, heads, 1)
+        rep[:, 0] = jnp.where(low, new, turned)
+        rep[:, 1] = jnp.where(low, turned, new)
+
+    row_slot = lax.broadcasted_iota(jnp.int32, (16, hd), 0) // heads
+
+    def put_rows(buf, rep, c):
+        for b in range(c * per, (c + 1) * per):
+            slot = lens_ref[b] - base
+
+            @pl.when((slot >= 0) & (slot < slots))
+            def _():
+                span = pl.ds(pl.multiple_of(slot // 4 * 16, 16), 16)
+                old = buf[b, span, :].astype(jnp.float32)
+                new = jnp.concatenate([rep[b // 2, b % 2]] * 2, axis=0)
+                buf[b, span, :] = jnp.where(row_slot == lax.rem(slot, 4), new, old).astype(buf.dtype)
+
+    q_t = qkv_ref[0].T.astype(jnp.bfloat16)
+    lane = lax.broadcasted_iota(jnp.int32, (1, 128), 1)
+    lane_seq, lane_head = lane // heads, lax.rem(lane, heads)
+    group = 128 // heads
+    row = lax.broadcasted_iota(jnp.int32, (pairs, 128), 0)
+    pos = base + row // heads
+    same_head = lax.rem(row, heads) == lane_head
+    slope = jnp.exp2((lax.axis_index("tp") * heads + lane_head + 1).astype(jnp.float32) * (-8.0 / all_heads))
+    per_group = chunks // (batch // group)
+    for g in range(batch // group):
+        q_g = q_t[:, g * 128:(g + 1) * 128]
+        scores = None
+        for c in range(g * per_group, (g + 1) * per_group):
+            moves(k_hbm, kbuf, k_in, c).wait()
+            put_rows(kbuf, rep_k, c)
+            seqs = range(c * per, (c + 1) * per)
+            keys = jnp.concatenate([kbuf[b] for b in seqs], axis=1)
+            query = jnp.concatenate([jnp.where(lane_seq == b - g * group, q_g, 0) for b in seqs], axis=0)
+            part = jnp.dot(keys, query, preferred_element_type=jnp.float32)
+            scores = part if scores is None else scores + part
+            moves(kbuf, kn_hbm, k_out, c).start()
+        length = jnp.zeros((1, 128), jnp.int32)
+        for i in range(group):
+            length = jnp.where(lane_seq == i, lens_ref[g * group + i], length)
+        scores = scores * hd ** -0.5 - slope * (length - pos).astype(jnp.float32)
+        valid = same_head & (pos <= length)
+        scores = jnp.where(valid, scores, -1e30)
+        top = jnp.max(scores, axis=0, keepdims=True)
+        p = jnp.where(valid, jnp.exp(scores - top), 0.0)
+        total = jnp.sum(p, axis=0, keepdims=True)
+        stats = jnp.concatenate([top, total, jnp.zeros((6, 128), jnp.float32)], axis=0)
+        for s in range(g * sp // (batch // group), (g + 1) * sp // (batch // group)):
+            pay_ref[s, batch // sp * heads:, :] = stats
+        p_t[g * 128:(g + 1) * 128, :] = p.T.astype(jnp.bfloat16)
+
+    quad = 16 // heads
+    row_seq = lax.broadcasted_iota(jnp.int32, (16, hd), 0) // heads
+    for c in range(chunks):
+        moves(v_hbm, vbuf, v_in, c).wait()
+        put_rows(vbuf, rep_v, c)
+        for b in range(c * per, (c + 1) * per, quad):
+            values = jnp.concatenate([vbuf[b + i] for i in range(quad)], axis=1)
+            out = jnp.dot(p_t[b * heads:b * heads + 16, :], values, preferred_element_type=jnp.float32)
+            out = sum(jnp.where(row_seq == i, out[:, i * hd:(i + 1) * hd], 0.0) for i in range(quad))
+            owner = b * sp // batch
+            at = (b - owner * (batch // sp)) * heads
+            pay_ref[owner, at:at + 16, :] = out
+        moves(vbuf, vn_hbm, v_out, c).start()
+    for c in range(chunks):
+        moves(kbuf, kn_hbm, k_out, c).wait()
+        moves(vbuf, vn_hbm, v_out, c).wait()
+
+
+def attend(tp, sp, lens, qkv, k_cache, v_cache):
+    batch, slots, heads, hd = k_cache.shape
+    chunks = 8
+    flat = (batch, slots * heads, hd)
+    vmem = pl.BlockSpec(memory_space=pltpu.VMEM)
+    hbm = pl.BlockSpec(memory_space=pl.ANY)
+    dma = pltpu.SemaphoreType.DMA
+    pay, k_next, v_next = pl.pallas_call(
+        functools.partial(attend_kernel, heads=heads, all_heads=heads * tp, sp=sp, chunks=chunks),
+        out_shape=(jax.ShapeDtypeStruct((sp, batch // sp * heads + 8, hd), jnp.float32),
+                   jax.ShapeDtypeStruct(flat, k_cache.dtype), jax.ShapeDtypeStruct(flat, v_cache.dtype)),
+        in_specs=[pl.BlockSpec(memory_space=pltpu.SMEM), vmem, hbm, hbm],
+        out_specs=(vmem, hbm, hbm),
+        scratch_shapes=[
+            pltpu.VMEM(flat, k_cache.dtype), pltpu.VMEM(flat, v_cache.dtype),
+            pltpu.VMEM((batch // 2, 2, 8, hd), jnp.float32), pltpu.VMEM((batch // 2, 2, 8, hd), jnp.float32),
+            pltpu.VMEM((batch * heads, slots * heads), jnp.bfloat16),
+            dma((chunks,)), dma((chunks,)), dma((chunks,)), dma((chunks,)),
+        ],
+        compiler_params=pltpu.CompilerParams(vmem_limit_bytes=60 * 2 ** 20),
+        name="attend",
+    )(lens, qkv, k_cache.reshape(flat), v_cache.reshape(flat))
+    return pay, k_next.reshape(k_cache.shape), v_next.reshape(v_cache.shape)
 
 
 def solution(mesh):
@@ -198,32 +311,13 @@
     sp_size = mesh.shape["sp"]
 
     def local_layer(x_in, seq_lens, k_cache, v_cache, ln1_gain, w_qkv, w_out, ln2_gain, w_up, w_down):
-        tok_dev = k_cache.shape[1]
+        batch = x_in.shape[0]
         local_heads = k_cache.shape[2]
         head_dim = k_cache.shape[3]
-        heads = local_heads * tp_size
-        tp_index = lax.axis_index("tp")
-        sp_index = lax.axis_index("sp")
         normed = layer_norm(x_in.astype(jnp.float32), ln1_gain).astype(jnp.bfloat16)
-        qkv_proj = jnp.einsum("bd,dchk->bchk", normed, w_qkv, preferred_element_type=jnp.float32).astype(jnp.bfloat16)
-        slot_pos = sp_index * tok_dev + jnp.arange(tok_dev)
-        slot_hit = (slot_pos[None, :] == seq_lens[:, None])[:, :, None, None]
-        k_next = jnp.where(slot_hit, qkv_proj[:, 1][:, None], k_cache)
-        v_next = jnp.where(slot_hit, qkv_proj[:, 2][:, None], v_cache)
-        head_ids = tp_index * local_heads + jnp.arange(local_heads)
-        slopes = jnp.exp2(-8.0 * (head_ids + 1).astype(jnp.float32) / heads)
-        scores = jnp.einsum("bhk,bthk->bht", qkv_proj[:, 0], k_next, preferred_element_type=jnp.float32) * head_dim ** -0.5
-        distance = (seq_lens[:, None] - slot_pos[None, :]).astype(jnp.float32)
-        scores = scores - slopes[None, :, None] * distance[:, None, :]
-        is_valid = (slot_pos[None, :] <= seq_lens[:, None])[:, None, :]
-        scores = jnp.where(is_valid, scores, -1e30)
-        local_max = jnp.max(scores, axis=2)
-        weights = jnp.where(is_valid, jnp.exp(scores - local_max[:, :, None]), 0.0)
-        local_sum = jnp.sum(weights, axis=2)
-        local_out = jnp.einsum("bht,bthk->bhk", weights.astype(jnp.bfloat16), v_next, preferred_element_type=jnp.float32)
-        batch = x_in.shape[0]
-        filler = jnp.zeros((batch, 128 - 2 * local_heads), jnp.float32)
-        pay = jnp.concatenate([local_out.reshape(batch, -1), local_max, local_sum, filler], axis=1)
+        qkv_proj = jnp.einsum("bd,dchk->cbhk", normed, w_qkv, preferred_element_type=jnp.float32).astype(jnp.bfloat16)
+        qkv_proj = qkv_proj.astype(jnp.float32).reshape(3, batch * local_heads, head_dim)
+        pay, k_next, v_next = attend(tp_size, sp_size, seq_lens, qkv_proj, k_cache, v_cache)
         x_out = tail(tp_size, sp_size, local_heads, head_dim, pay, x_in, ln2_gain, w_out, w_up, w_down)
         return x_out, k_next, v_next
 

time: 78 us -> 58.3 us (0.75)
  other arithmetic: 18.3 us -> 2.29 us
  Pallas kernels: 33.1 us -> 48.3 us
  matrix products: 14.2 us -> 4.16 us
  local copies, waits for them, and re-layouts: 11.3 us -> 2.66 us
    pallas_call x0 -> x1, Pallas kernels: none -> 14 us  [attend(): pl.pallas_call(functools.partial(attend_kernel, heads=heads, all_heads=he...]
    select_n x1 -> x0, other arithmetic: 13.7 us -> none  [local_layer(): v_next = jnp.where(slot_hit, qkv_proj[:, 2][:, None], v_cache)]
    dot_general x3 -> x1, matrix products: 14.2 us -> 4.16 us  [local_layer(): jnp.einsum('bd,dchk->cbhk', normed, w_qkv, preferred_element_type=jnp.flo...]
    unnamed x16 -> x1, local copies, waits for them, and re-layouts: 10.9 us -> 1.67 us
    pallas_call x1, Pallas kernels: 33.1 us -> 34.3 us  [tail(): pl.pallas_call(functools.partial(tail_kernel, tp, sp, heads, hd), out_sha...]
    reshape x0 -> x1, local copies, waits for them, and re-layouts: none -> 0.99 us  [local_layer(): qkv_proj.astype(jnp.float32).reshape(3, batch * local_heads, head_dim)]
    convert_element_type x2 -> x0, other arithmetic: 0.93 us -> none  [the longest x1 0.73 us: local_layer(): distance = (seq_lens[:, None] - slot_pos[None, :]).astype(jnp.float32)]
where the time goes in v2:
time: 58.3 us; the launch traced here: 58.1 us
  Pallas kernels  48.3 us (83%)
  matrix products  4.16 us (7%)
  local copies, waits for them, and re-layouts  2.66 us (5%)
  other arithmetic  2.29 us (4%)
  between operations  0.68 us (1%)
    pallas_call x1, Pallas kernels, tail(): pl.pallas_call(functools.partial(tail_kernel, tp, sp, heads, hd), out_sha...  34.3 us
    pallas_call x1, Pallas kernels, attend(): pl.pallas_call(functools.partial(attend_kernel, heads=heads, all_heads=he...  14 us
    dot_general x1, matrix products, local_layer(): jnp.einsum('bd,dchk->cbhk', normed, w_qkv, preferred_element_type=jnp.flo...  4.16 us
    unnamed x1, local copies, waits for them, and re-layouts  1.67 us
    reduce_sum x1, other arithmetic, layer_norm(): variance = jnp.mean(centred * centred, axis=-1, keepdims=True)  1.19 us

profile of v2, /device:TPU:0, one launch (start us, length us, event | category | flops | bytes accessed | tf_op | source)
XLA Modules:
  0.0 58.1 jit_solution(12476358163576897859)
XLA Ops:
  0.6 1.1 %convert_reduce_fusion = f32[64]{0:T(128)S(1)} fusion(bf16[64,2048]{1,0:T(8,128)(2,1)} %x_ref.1), kind=kLoop, calls=%fused_computation.6 | loop fusion | flops 262080 | bytes 262400 | tf_op jit(solution)/shard_map/reduce_sum | solution.py:15
  1.7 1.2 %fusion.13 = f32[64]{0:T(128)S(1)} fusion(bf16[64,2048]{1,0:T(8,128)(2,1)} %x_ref.1, f32[64]{0:T(128)S(1)} %broadcast_multiply_fusion), kind=kLoop, calls=%fused_computation.9 | loop fusion | flops 524224 | bytes 262656 | tf_op jit(solution)/shard_map/reduce_sum | solution.py:17
  2.9 4.2 %fusion.8 = f32[3,64,4,128]{3,1,2,0:T(8,128)S(1)} fusion(bf16[2048,3,4,128]{3,2,1,0:T(4,128)(2,1)} %param.15, bf16[64,2048]{1,0:T(8,128)(2,1)} %x_ref.1, f32[2048]{0:T(1024)} %param.14, f32[64]{0:T(128)S(1)} %add_rsqrt_fusion, f32[64]{0:T(128)S(1)} %broadcast_multiply_fusion), kind=kOutput, calls=%fused_computation.4 | convolution fusion | flops 403505152 | bytes 6955520 | tf_op jit(solution)/shard_map/bd,dchk->cbhk/dot_general | solution.py:318
  7.1 1.0 %copy.14 = f32[3,64,4,128]{3,2,1,0:T(4,128)} copy(f32[3,64,4,128]{3,1,2,0:T(8,128)S(1)} %fusion.8) | data formatting | bytes 786432 | tf_op jit(solution)/shard_map/reshape | solution.py:319
  8.1 14.0 %attend.1 = (f32[4,72,128]{2,1,0:T(8,128)}, bf16[64,512,128]{2,1,0:T(8,128)(2,1)}, bf16[64,512,128]{2,1,0:T(8,128)(2,1)}) custom-call(s32[64]{0:T(128)} %lens_ref.1, f32[3,256,128]{2,1,0:T(8,128)} %bitcast.17, bf16[64,512,128]{2,1,0:T(8,128)(2,1)} %bitcast.14, bf16[64,512,128]{2,1,0:T(8,128)(2,1)} %bitcast.15), custom_call_target="tpu_custom_call" | custom-call | tf_op jit(solution)/shard_map/attend/pallas_call | solution.py:291
  22.1 34.3 %tail.1 = bf16[64,2048]{1,0:T(8,128)(2,1)} custom-call(f32[4,72,128]{2,1,0:T(8,128)} %get-tuple-element.6.pay_ref, bf16[64,2048]{1,0:T(8,128)(2,1)} %x_ref.1, f32[1,2048]{1,0:T(1,128)} %bitcast.18, bf16[512,2048]{1,0:T(8,128)(2,1)} %bitcast.16, bf16[2048,2048]{1,0:T(8,128)(2,1)} %wu_hbm.1, bf16[2048,2048]{1,0:T(8,128)(2,1)} %wd_hbm.1), custom_call_target="tpu_custom_call" | custom-call | tf_op jit(solution)/shard_map/tail/pallas_call | solution.py:167
  56.4 1.7 %copy.25 = bf16[64,2048]{1,0:T(8,128)(2,1)} copy(bf16[64,2048]{1,0:T(8,128)(2,1)} %tail.1) | data formatting | bytes 524288
  (2 shorter events, 0.0 us)

commit v3 on v2

--- a/solution.py
+++ b/solution.py
@@ -162,7 +162,7 @@
     ff = w_up.shape[1]
     width = heads * hd
     vmem = pl.BlockSpec(memory_space=pltpu.VMEM)
-    hbm = pl.BlockSpec(memory_space=pl.ANY)
+    hbm = pl.BlockSpec(memory_space=pltpu.HBM)
     dma = pltpu.SemaphoreType.DMA
     return pl.pallas_call(
         functools.partial(tail_kernel, tp, sp, heads, hd),
@@ -187,13 +187,14 @@
             dma((sp,)), dma((sp,)), dma((tp,)), dma((tp,)), dma((tp,)), dma((tp,)), dma((tp,)), dma((tp,)),
             dma((tp,)), dma((tp,)), dma((2 * tp,)), dma((sp, tp)),
         ],
-        compiler_params=pltpu.CompilerParams(collective_id=0, has_side_effects=True, vmem_limit_bytes=60 * 2 ** 20),
+        compiler_params=pltpu.CompilerParams(collective_id=0, has_side_effects=True, vmem_limit_bytes=24 * 2 ** 20),
         name="tail",
-    )(pay, x_in, gain[None, :], w_out.reshape(width, d), w_up, w_down)
-
-
-def attend_kernel(lens_ref, qkv_ref, k_hbm, v_hbm, pay_ref, kn_hbm, vn_hbm,
-                  kbuf, vbuf, rep_k, rep_v, p_t, k_in, v_in, k_out, v_out, *, heads, all_heads, sp, chunks):
+    )(pay, x_in, gain[None, :], *(pltpu.with_memory_space_constraint(w, pltpu.HBM) for w in (w_out.reshape(width, d), w_up, w_down)))
+
+
+def attend_kernel(lens_hbm, x_hbm, gain_hbm, w_hbm, k_hbm, v_hbm, pay_ref, kn_hbm, vn_hbm,
+                  lens_ref, x_ref, gain_ref, wbuf, wide, normed, qkv, kbuf, vbuf, rep_k, rep_v, p_t,
+                  small_in, w_in, k_in, v_in, k_out, v_out, *, heads, all_heads, sp, chunks):
     batch, pairs, hd = kbuf.shape
     slots = pairs // heads
     per = batch // chunks
@@ -203,14 +204,42 @@
         part = pl.ds(c * per, per)
         return pltpu.make_async_copy(src.at[part], dst.at[part], sem.at[c])
 
-    for c in range(chunks):
-        moves(k_hbm, kbuf, k_in, c).start()
-    for c in range(chunks):
-        moves(v_hbm, vbuf, v_in, c).start()
+    small = [pltpu.make_async_copy(src, dst, small_in.at[i])
+             for i, (src, dst) in enumerate(((x_hbm, x_ref), (gain_hbm, gain_ref), (lens_hbm, lens_ref)))]
+    for copy in small:
+        copy.start()
+    d = x_ref.shape[1]
+    parts = 3 * heads
+    depth = wide.shape[0] // parts
+    pieces = d // depth
+    w_copies = []
+    for j in range(pieces):
+        part = pl.ds(j * depth * parts, depth * parts)
+        w_copies.append(pltpu.make_async_copy(w_hbm.at[part], wbuf.at[part], w_in.at[j]))
+        w_copies[j].start()
+    moves(k_hbm, kbuf, k_in, 0).start()
+
+    for copy in small:
+        copy.wait()
+    normed[...] = layer_norm(x_ref[...].astype(jnp.float32), gain_ref[...]).astype(jnp.bfloat16)
+    proj = None
+    for j in range(pieces):
+        w_copies[j].wait()
+        if j + 1 < chunks:
+            moves(k_hbm, kbuf, k_in, j + 1).start()
+        else:
+            moves(v_hbm, vbuf, v_in, 0).start()
+        wide[...] = wbuf[j * depth * parts:(j + 1) * depth * parts, :].astype(jnp.float32)
+        w = jnp.concatenate([wide[pl.ds(i, depth, stride=parts), :].astype(jnp.bfloat16) for i in range(parts)], axis=1)
+        part = jnp.dot(normed[:, j * depth:(j + 1) * depth], w, preferred_element_type=jnp.float32)
+        proj = part if proj is None else proj + part
+    for i in range(parts):
+        qkv[i // heads, pl.ds(i % heads, batch, stride=heads), :] = (
+            proj[:, i * hd:(i + 1) * hd].astype(jnp.bfloat16).astype(jnp.float32))
 
     low = lax.broadcasted_iota(jnp.int32, (1, 8, hd), 1) < heads
     for rep, i in ((rep_k, 1), (rep_v, 2)):
-        new = qkv_ref[i].reshape(batch // 2, 8, hd)
+        new = qkv[i].reshape(batch // 2, 8, hd)
         turned = pltpu.roll(new, heads, 1)
         rep[:, 0] = jnp.where(low, new, turned)
         rep[:, 1] = jnp.where(low, turned, new)
@@ -228,7 +257,7 @@
                 new = jnp.concatenate([rep[b // 2, b % 2]] * 2, axis=0)
                 buf[b, span, :] = jnp.where(row_slot == lax.rem(slot, 4), new, old).astype(buf.dtype)
 
-    q_t = qkv_ref[0].T.astype(jnp.bfloat16)
+    q_t = qkv[0].T.astype(jnp.bfloat16)
     lane = lax.broadcasted_iota(jnp.int32, (1, 128), 1)
     lane_seq, lane_head = lane // heads, lax.rem(lane, heads)
     group = 128 // heads
@@ -242,6 +271,8 @@
         scores = None
         for c in range(g * per_group, (g + 1) * per_group):
             moves(k_hbm, kbuf, k_in, c).wait()
+            if c + 1 < chunks:
+                moves(v_hbm, vbuf, v_in, c + 1).start()
             put_rows(kbuf, rep_k, c)
             seqs = range(c * per, (c + 1) * per)
             keys = jnp.concatenate([kbuf[b] for b in seqs], axis=1)
@@ -281,28 +312,33 @@
         moves(vbuf, vn_hbm, v_out, c).wait()
 
 
-def attend(tp, sp, lens, qkv, k_cache, v_cache):
+def attend(tp, sp, lens, x_in, gain, w_qkv, k_cache, v_cache):
     batch, slots, heads, hd = k_cache.shape
-    chunks = 8
+    d = x_in.shape[1]
+    chunks, pieces = 8, 8
     flat = (batch, slots * heads, hd)
     vmem = pl.BlockSpec(memory_space=pltpu.VMEM)
-    hbm = pl.BlockSpec(memory_space=pl.ANY)
+    hbm = pl.BlockSpec(memory_space=pltpu.HBM)
     dma = pltpu.SemaphoreType.DMA
+    operands = (lens, x_in, gain[None, :], w_qkv.reshape(d * 3 * heads, hd), k_cache.reshape(flat), v_cache.reshape(flat))
     pay, k_next, v_next = pl.pallas_call(
         functools.partial(attend_kernel, heads=heads, all_heads=heads * tp, sp=sp, chunks=chunks),
         out_shape=(jax.ShapeDtypeStruct((sp, batch // sp * heads + 8, hd), jnp.float32),
                    jax.ShapeDtypeStruct(flat, k_cache.dtype), jax.ShapeDtypeStruct(flat, v_cache.dtype)),
-        in_specs=[pl.BlockSpec(memory_space=pltpu.SMEM), vmem, hbm, hbm],
+        in_specs=[hbm] * len(operands),
         out_specs=(vmem, hbm, hbm),
         scratch_shapes=[
+            pltpu.SMEM(lens.shape, lens.dtype), pltpu.VMEM(x_in.shape, x_in.dtype), pltpu.VMEM((1, d), gain.dtype),
+            pltpu.VMEM((d * 3 * heads, hd), jnp.bfloat16), pltpu.VMEM((d // pieces * 3 * heads, hd), jnp.float32),
+            pltpu.VMEM((batch, d), jnp.bfloat16), pltpu.VMEM((3, batch * heads, hd), jnp.float32),
             pltpu.VMEM(flat, k_cache.dtype), pltpu.VMEM(flat, v_cache.dtype),
             pltpu.VMEM((batch // 2, 2, 8, hd), jnp.float32), pltpu.VMEM((batch // 2, 2, 8, hd), jnp.float32),
             pltpu.VMEM((batch * heads, slots * heads), jnp.bfloat16),
-            dma((chunks,)), dma((chunks,)), dma((chunks,)), dma((chunks,)),
+            dma((3,)), dma((pieces,)), dma((chunks,)), dma((chunks,)), dma((chunks,)), dma((chunks,)),
         ],
-        compiler_params=pltpu.CompilerParams(vmem_limit_bytes=60 * 2 ** 20),
+        compiler_params=pltpu.CompilerParams(vmem_limit_bytes=36 * 2 ** 20),
         name="attend",
-    )(lens, qkv, k_cache.reshape(flat), v_cache.reshape(flat))
+    )(*(pltpu.with_memory_space_constraint(a, pltpu.HBM) for a in operands))
     return pay, k_next.reshape(k_cache.shape), v_next.reshape(v_cache.shape)
 
 
@@ -311,13 +347,9 @@
     sp_size = mesh.shape["sp"]
 
     def local_layer(x_in, seq_lens, k_cache, v_cache, ln1_gain, w_qkv, w_out, ln2_gain, w_up, w_down):
-        batch = x_in.shape[0]
         local_heads = k_cache.shape[2]
         head_dim = k_cache.shape[3]
-        normed = layer_norm(x_in.astype(jnp.float32), ln1_gain).astype(jnp.bfloat16)
-        qkv_proj = jnp.einsum("bd,dchk->cbhk", normed, w_qkv, preferred_element_type=jnp.float32).astype(jnp.bfloat16)
-        qkv_proj = qkv_proj.astype(jnp.float32).reshape(3, batch * local_heads, head_dim)
-        pay, k_next, v_next = attend(tp_size, sp_size, seq_lens, qkv_proj, k_cache, v_cache)
+        pay, k_next, v_next = attend(tp_size, sp_size, seq_lens, x_in, ln1_gain, w_qkv, k_cache, v_cache)
         x_out = tail(tp_size, sp_size, local_heads, head_dim, pay, x_in, ln2_gain, w_out, w_up, w_down)
         return x_out, k_next, v_next
 

time: 58.3 us -> 49.6 us (0.85)
  matrix products: 4.16 us -> 0 us
  other arithmetic: 2.29 us -> 0 us
  local copies, waits for them, and re-layouts: 2.66 us -> 0.71 us
  Pallas kernels: 48.3 us -> 47.6 us
    dot_general x1 -> x0, matrix products: 4.16 us -> none  [local_layer(): jnp.einsum('bd,dchk->cbhk', normed, w_qkv, preferred_element_type=jnp.flo...]
    reduce_sum x2 -> x0, other arithmetic: 2.28 us -> none  [the longest x1 1.19 us: layer_norm(): variance = jnp.mean(centred * centred, axis=-1, keepdims=True)]
    pallas_call x1, Pallas kernels: 34.3 us -> 32.6 us  [tail(): pl.pallas_call(functools.partial(tail_kernel, tp, sp, heads, hd), out_sha...]
    pallas_call x1, Pallas kernels: 14 us -> 15 us  [attend(): pl.pallas_call(functools.partial(attend_kernel, heads=heads, all_heads=he...]
    reshape x1 -> x0, local copies, waits for them, and re-layouts: 0.99 us -> none  [local_layer(): qkv_proj.astype(jnp.float32).reshape(3, batch * local_heads, head_dim)]
    unnamed x1 -> x5, local copies, waits for them, and re-layouts: 1.67 us -> 0.71 us
where the time goes in v3:
time: 49.6 us; the launch traced here: 49 us
  Pallas kernels  47.6 us (96%)
  local copies, waits for them, and re-layouts  0.71 us (1%)
  between operations  0.68 us (1%)
    pallas_call x1, Pallas kernels, tail(): pl.pallas_call(functools.partial(tail_kernel, tp, sp, heads, hd), out_sha...  32.6 us
    pallas_call x1, Pallas kernels, attend(): pl.pallas_call(functools.partial(attend_kernel, heads=heads, all_heads=he...  15 us

profile of v3, /device:TPU:0, one launch (start us, length us, event | category | flops | bytes accessed | tf_op | source)
XLA Modules:
  0.0 49.0 jit_solution(4622923053141770926)
XLA Ops:
  0.6 0.0 copy-start
  0.6 0.0 copy-start.1
  0.7 15.0 %attend.1 = (f32[4,72,128]{2,1,0:T(8,128)S(1)}, bf16[64,512,128]{2,1,0:T(8,128)(2,1)}, bf16[64,512,128]{2,1,0:T(8,128)(2,1)}) custom-call(s32[64]{0:T(128)} %lens_hbm.1, bf16[64,2048]{1,0:T(8,128)(2,1)} %x_ref.1, f32[1,2048]{1,0:T(1,128)} %bitcast.13, bf16[24576,128]{1,0:T(8,128)(2,1)} %bitcast.11, bf16[64,512,128]{2,1,0:T(8,128)(2,1)} %bitcast.9, ...), custom_call_target="tpu_custom_call" | custom-call | tf_op jit(solution)/shard_map/attend/pallas_call | solution.py:324
  15.7 0.0 copy-done
  15.7 0.0 copy-done.1
  15.7 32.6 %tail.1 = bf16[64,2048]{1,0:T(8,128)(2,1)S(1)} custom-call(f32[4,72,128]{2,1,0:T(8,128)S(1)} %get-tuple-element.6.pay_ref, bf16[64,2048]{1,0:T(8,128)(2,1)S(1)} %copy-done, f32[1,2048]{1,0:T(1,128)S(1)} %bitcast.8, bf16[512,2048]{1,0:T(8,128)(2,1)} %bitcast.12, bf16[2048,2048]{1,0:T(8,128)(2,1)} %wu_hbm.1, bf16[2048,2048]{1,0:T(8,128)(2,1)} %wd_hbm.1), custom_call_target="tpu_custom_call" | custom-call | tf_op jit(solution)/shard_map/tail/pallas_call | solution.py:167
  48.3 0.7 %copy.14 = bf16[64,2048]{1,0:T(8,128)(2,1)} copy(bf16[64,2048]{1,0:T(8,128)(2,1)S(1)} %tail.1) | data formatting | bytes 524288
Async XLA Ops:
  0.6 15.0 %copy-start = (bf16[64,2048]{1,0:T(8,128)(2,1)S(1)}, bf16[64,2048]{1,0:T(8,128)(2,1)}, u32[]{:S(2)}) copy-start(bf16[64,2048]{1,0:T(8,128)(2,1)} %x_ref.1) | copy-start | bytes 786436
  0.6 15.0 %copy-start.1 = (f32[2048]{0:T(1024)S(1)}, f32[2048]{0:T(1024)}, u32[]{:S(2)}) copy-start(f32[2048]{0:T(1024)} %param.17) | copy-start | bytes 24580

commit v4 on v3

--- a/solution.py
+++ b/solution.py
@@ -71,87 +71,88 @@
     att[...] = sum(coef[:, i:i + 1] * b[:pairs] for i, b in enumerate(blocks)) / coef[:, sp:sp + 1]
     attended = jnp.concatenate([att[pl.ds(h, rows, stride=heads), :] for h in range(heads)], axis=1).astype(jnp.bfloat16)
 
+    high = my_tp // 2
+    near = (my_tp + 1 - 2 * lax.rem(my_tp, 2), 2 - high, 3 - 3 * high)
+    far = near[::-1]
+    split = part.shape[1]
+    piece = cols // split
+
+    def send(src, dst, send_sem, recv_sem, to):
+        copy = pltpu.make_async_remote_copy(src, dst, send_sem, recv_sem, device_id=to, device_id_type=MESH)
+        copy.start()
+        sends.append(copy)
+
+    def reduce_scatter(lhs, weights, buf, got, send_sem, recv_sem):
+        for i in range(split):
+            for peer in far:
+                buf[peer, i] = jnp.dot(lhs, weights[peer, :, i * piece:(i + 1) * piece], preferred_element_type=jnp.float32)
+                send(buf.at[peer, i], got.at[my_tp, i], send_sem.at[peer, i], recv_sem.at[my_tp, i], {"tp": peer})
+        own = [jnp.dot(lhs, weights[my_tp, :, i * piece:(i + 1) * piece], preferred_element_type=jnp.float32)
+               for i in range(split)]
+
+        def total(i):
+            out = own[i]
+            for peer in near:
+                arrived(got.at[peer, i], recv_sem.at[peer, i])
+                out += got[peer, i]
+            return out
+        return total
+
     for j in range(tp):
         loads["o", j].wait()
-    for off in range(1, tp):
-        peer = lax.rem(my_tp + off, tp)
-        part[peer] = jnp.dot(attended, wo[peer], preferred_element_type=jnp.float32)
-        copy = pltpu.make_async_remote_copy(part.at[peer], got_part.at[my_tp], s2.at[off], r2.at[my_tp],
-                                            device_id={"tp": peer}, device_id_type=MESH)
-        copy.start()
-        sends.append(copy)
-    mine = jnp.dot(attended, wo[my_tp], preferred_element_type=jnp.float32)
+    total = reduce_scatter(attended, wo, part, got_part, s2, r2)
     row0 = pl.multiple_of(my_sp * rows, rows)
-    mine += x_ref[pl.ds(row0, rows), pl.ds(pl.multiple_of(my_tp * cols, cols), cols)].astype(jnp.float32)
-    for off in range(1, tp):
-        peer = lax.rem(my_tp + off, tp)
-        arrived(got_part.at[peer], r2.at[peer])
-        mine += got_part[peer]
-    r_all[my_tp] = mine
-    for off in range(1, tp):
-        peer = lax.rem(my_tp + off, tp)
-        copy = pltpu.make_async_remote_copy(r_all.at[my_tp], r_all.at[my_tp], s3.at[off], r3.at[my_tp],
-                                            device_id={"tp": peer}, device_id_type=MESH)
-        copy.start()
-        sends.append(copy)
-    for off in range(1, tp):
-        peer = lax.rem(my_tp + off, tp)
-        arrived(r_all.at[peer], r3.at[peer])
-
-    r = jnp.concatenate([r_all[j] for j in range(tp)], axis=1)
+    for i in range(split):
+        col0 = pl.multiple_of(my_tp * cols + i * piece, piece)
+        r_all[my_tp, i] = total(i) + x_ref[pl.ds(row0, rows), pl.ds(col0, piece)].astype(jnp.float32)
+        for peer in far:
+            send(r_all.at[my_tp, i], r_all.at[my_tp, i], s3.at[peer, i], r3.at[my_tp, i], {"tp": peer})
+    for i in range(split):
+        for peer in near:
+            arrived(r_all.at[peer, i], r3.at[peer, i])
+
+    r = jnp.concatenate([r_all[j, i] for j in range(tp) for i in range(split)], axis=1)
     h_mid[...] = layer_norm(r, gain_ref[...]).astype(jnp.bfloat16)
 
     for j in range(tp):
         loads["u", j].wait()
         up = jnp.dot(h_mid[...], wu[j], preferred_element_type=jnp.float32)
-        hidden[:, j * cols:(j + 1) * cols] = gelu(up).astype(jnp.bfloat16)
+        hidden[:, j * wu.shape[2]:(j + 1) * wu.shape[2]] = gelu(up).astype(jnp.bfloat16)
 
     for j in range(tp):
         loads["d", j].wait()
-    for off in range(1, tp):
-        peer = lax.rem(my_tp + off, tp)
-        down[peer] = jnp.dot(hidden[...], wd[peer], preferred_element_type=jnp.float32)
-        copy = pltpu.make_async_remote_copy(down.at[peer], got_down.at[my_tp], s4.at[off], r4.at[my_tp],
-                                            device_id={"tp": peer}, device_id_type=MESH)
-        copy.start()
-        sends.append(copy)
-    mine = r_all[my_tp] + jnp.dot(hidden[...], wd[my_tp], preferred_element_type=jnp.float32)
-    for off in range(1, tp):
-        peer = lax.rem(my_tp + off, tp)
-        arrived(got_down.at[peer], r4.at[peer])
-        mine += got_down[peer]
-    x_all[my_sp, my_tp] = mine.astype(jnp.bfloat16).astype(jnp.float32)
+    total = reduce_scatter(hidden[...], wd, down, got_down, s4, r4)
 
     side = lax.rem(my_sp + 2, sp)
     twin = my_sp + 1 - 2 * lax.rem(my_sp, 2)
     side_twin = lax.rem(twin + 2, sp)
 
-    def pass_on(s, t, send_sem, slot, to):
-        copy = pltpu.make_async_remote_copy(x_all.at[s, t], x_all.at[s, t], send_sem.at[slot], r5.at[s, t],
-                                            device_id=to, device_id_type=MESH)
-        copy.start()
-        sends.append(copy)
-
-    for off in range(1, tp):
-        pass_on(my_sp, my_tp, s5z, off, {"tp": lax.rem(my_tp + off, tp)})
-    pass_on(my_sp, my_tp, s5y, 0, {"sp": side})
-    pass_on(my_sp, my_tp, s5c, 0, {"sp": twin})
-    for off in range(1, tp):
-        peer = lax.rem(my_tp + off, tp)
-        arrived(x_all.at[my_sp, peer], r5.at[my_sp, peer])
-        pass_on(my_sp, peer, s5y, off, {"sp": side})
-        pass_on(my_sp, peer, s5c, off, {"sp": twin})
-    for off in range(tp):
-        peer = lax.rem(my_tp + off, tp)
-        arrived(x_all.at[side, peer], r5.at[side, peer])
-        pass_on(side, peer, s5c, tp + off, {"sp": twin})
+    def pass_on(s, t, i, send_sem, to):
+        send(x_all.at[s, t, i], x_all.at[s, t, i], send_sem, r5.at[s, t, i], to)
+
+    for i in range(split):
+        x_all[my_sp, my_tp, i] = (r_all[my_tp, i] + total(i)).astype(jnp.bfloat16).astype(jnp.float32)
+        for peer in far:
+            pass_on(my_sp, my_tp, i, s5y.at[peer, i], {"tp": peer, "sp": side})
+            pass_on(my_sp, my_tp, i, s5z.at[peer, i], {"tp": peer})
+        pass_on(my_sp, my_tp, i, s5y.at[my_tp, i], {"sp": side})
+        pass_on(my_sp, my_tp, i, s5c.at[0, my_tp, i], {"sp": twin})
+    for i in range(split):
+        arrived(x_all.at[side, my_tp, i], r5.at[side, my_tp, i])
+        pass_on(side, my_tp, i, s5c.at[1, my_tp, i], {"sp": twin})
+        for peer in near:
+            for n, who in enumerate((my_sp, side)):
+                arrived(x_all.at[who, peer, i], r5.at[who, peer, i])
+                pass_on(who, peer, i, s5c.at[n, peer, i], {"sp": twin})
     for who in (twin, side_twin):
-        for off in range(tp):
-            peer = lax.rem(my_tp + off, tp)
-            arrived(x_all.at[who, peer], r5.at[who, peer])
+        for i in range(split):
+            for peer in (my_tp,) + near:
+                arrived(x_all.at[who, peer, i], r5.at[who, peer, i])
     for s in range(sp):
         for t in range(tp):
-            out_ref[s * rows:(s + 1) * rows, t * cols:(t + 1) * cols] = x_all[s, t].astype(jnp.bfloat16)
+            for i in range(split):
+                at = t * cols + i * piece
+                out_ref[s * rows:(s + 1) * rows, at:at + piece] = x_all[s, t, i].astype(jnp.bfloat16)
     for copy in sends:
         copy.wait_send()
 
@@ -159,6 +160,8 @@
 def tail(tp, sp, heads, hd, pay, x_in, gain, w_out, w_up, w_down):
     batch, d = x_in.shape
     rows, cols = batch // sp, d // tp
+    split = 1
+    blocks = (tp, split, rows, cols // split)
     ff = w_up.shape[1]
     width = heads * hd
     vmem = pl.BlockSpec(memory_space=pltpu.VMEM)
@@ -175,17 +178,13 @@
             pltpu.VMEM((tp, ff, cols), jnp.bfloat16),
             pltpu.VMEM(pay.shape, jnp.float32),
             pltpu.VMEM((rows * heads, hd), jnp.float32),
-            pltpu.VMEM((tp, rows, cols), jnp.float32),
-            pltpu.VMEM((tp, rows, cols), jnp.float32),
-            pltpu.VMEM((tp, rows, cols), jnp.float32),
+            pltpu.VMEM(blocks, jnp.float32), pltpu.VMEM(blocks, jnp.float32), pltpu.VMEM(blocks, jnp.float32),
             pltpu.VMEM((rows, d), jnp.bfloat16),
             pltpu.VMEM((rows, ff), jnp.bfloat16),
-            pltpu.VMEM((tp, rows, cols), jnp.float32),
-            pltpu.VMEM((tp, rows, cols), jnp.float32),
-            pltpu.VMEM((sp, tp, rows, cols), jnp.float32),
+            pltpu.VMEM(blocks, jnp.float32), pltpu.VMEM(blocks, jnp.float32),
+            pltpu.VMEM((sp,) + blocks, jnp.float32),
             dma((tp,)), dma((tp,)), dma((tp,)),
-            dma((sp,)), dma((sp,)), dma((tp,)), dma((tp,)), dma((tp,)), dma((tp,)), dma((tp,)), dma((tp,)),
-            dma((tp,)), dma((tp,)), dma((2 * tp,)), dma((sp, tp)),
+            dma((sp,)), dma((sp,)), *[dma((tp, split))] * 8, dma((2, tp, split)), dma((sp, tp, split)),
         ],
         compiler_params=pltpu.CompilerParams(collective_id=0, has_side_effects=True, vmem_limit_bytes=24 * 2 ** 20),
         name="tail",
@@ -194,7 +193,7 @@
 
 def attend_kernel(lens_hbm, x_hbm, gain_hbm, w_hbm, k_hbm, v_hbm, pay_ref, kn_hbm, vn_hbm,
                   lens_ref, x_ref, gain_ref, wbuf, wide, normed, qkv, kbuf, vbuf, rep_k, rep_v, p_t,
-                  small_in, w_in, k_in, v_in, k_out, v_out, *, heads, all_heads, sp, chunks):
+                  small_in, w_in, k_in, v_in, k_out, v_out, *, heads, all_heads, sp, chunks, ahead):
     batch, pairs, hd = kbuf.shape
     slots = pairs // heads
     per = batch // chunks
@@ -212,23 +211,25 @@
     parts = 3 * heads
     depth = wide.shape[0] // parts
     pieces = d // depth
-    w_copies = []
+    loads = []
     for j in range(pieces):
         part = pl.ds(j * depth * parts, depth * parts)
-        w_copies.append(pltpu.make_async_copy(w_hbm.at[part], wbuf.at[part], w_in.at[j]))
-        w_copies[j].start()
-    moves(k_hbm, kbuf, k_in, 0).start()
+        loads.append(pltpu.make_async_copy(w_hbm.at[part], wbuf.at[part], w_in.at[j]))
+    loads += [moves(k_hbm, kbuf, k_in, c) for c in range(chunks)] + [moves(v_hbm, vbuf, v_in, c) for c in range(chunks)]
+    for copy in loads[:ahead]:
+        copy.start()
+
+    def loaded(i):
+        loads[i].wait()
+        if i + ahead < len(loads):
+            loads[i + ahead].start()
 
     for copy in small:
         copy.wait()
     normed[...] = layer_norm(x_ref[...].astype(jnp.float32), gain_ref[...]).astype(jnp.bfloat16)
     proj = None
     for j in range(pieces):
-        w_copies[j].wait()
-        if j + 1 < chunks:
-            moves(k_hbm, kbuf, k_in, j + 1).start()
-        else:
-            moves(v_hbm, vbuf, v_in, 0).start()
+        loaded(j)
         wide[...] = wbuf[j * depth * parts:(j + 1) * depth * parts, :].astype(jnp.float32)
         w = jnp.concatenate([wide[pl.ds(i, depth, stride=parts), :].astype(jnp.bfloat16) for i in range(parts)], axis=1)
         part = jnp.dot(normed[:, j * depth:(j + 1) * depth], w, preferred_element_type=jnp.float32)
@@ -270,9 +271,7 @@
         q_g = q_t[:, g * 128:(g + 1) * 128]
         scores = None
         for c in range(g * per_group, (g + 1) * per_group):
-            moves(k_hbm, kbuf, k_in, c).wait()
-            if c + 1 < chunks:
-                moves(v_hbm, vbuf, v_in, c + 1).start()
+            loaded(pieces + c)
             put_rows(kbuf, rep_k, c)
             seqs = range(c * per, (c + 1) * per)
             keys = jnp.concatenate([kbuf[b] for b in seqs], axis=1)
@@ -297,7 +296,7 @@
     quad = 16 // heads
     row_seq = lax.broadcasted_iota(jnp.int32, (16, hd), 0) // heads
     for c in range(chunks):
-        moves(v_hbm, vbuf, v_in, c).wait()
+        loaded(pieces + chunks + c)
         put_rows(vbuf, rep_v, c)
         for b in range(c * per, (c + 1) * per, quad):
             values = jnp.concatenate([vbuf[b + i] for i in range(quad)], axis=1)
@@ -315,14 +314,14 @@
 def attend(tp, sp, lens, x_in, gain, w_qkv, k_cache, v_cache):
     batch, slots, heads, hd = k_cache.shape
     d = x_in.shape[1]
-    chunks, pieces = 8, 8
+    chunks, pieces, ahead = 4, 4, 4
     flat = (batch, slots * heads, hd)
     vmem = pl.BlockSpec(memory_space=pltpu.VMEM)
     hbm = pl.BlockSpec(memory_space=pltpu.HBM)
     dma = pltpu.SemaphoreType.DMA
     operands = (lens, x_in, gain[None, :], w_qkv.reshape(d * 3 * heads, hd), k_cache.reshape(flat), v_cache.reshape(flat))
     pay, k_next, v_next = pl.pallas_call(
-        functools.partial(attend_kernel, heads=heads, all_heads=heads * tp, sp=sp, chunks=chunks),
+        functools.partial(attend_kernel, heads=heads, all_heads=heads * tp, sp=sp, chunks=chunks, ahead=ahead),
         out_shape=(jax.ShapeDtypeStruct((sp, batch // sp * heads + 8, hd), jnp.float32),
                    jax.ShapeDtypeStruct(flat, k_cache.dtype), jax.ShapeDtypeStruct(flat, v_cache.dtype)),
         in_specs=[hbm] * len(operands),

time: 49.6 us -> 46.7 us (0.942)
  Pallas kernels: 47.6 us -> 45.2 us
    pallas_call x1, Pallas kernels: 32.6 us -> 31.1 us  [tail(): pl.pallas_call(functools.partial(tail_kernel, tp, sp, heads, hd), out_sha...]
    pallas_call x1, Pallas kernels: 15 us -> 14.1 us  [attend(): pl.pallas_call(functools.partial(attend_kernel, heads=heads, all_heads=he...]
where the time goes in v4:
time: 46.7 us; the launch traced here: 46.6 us
  Pallas kernels  45.2 us (97%)
  local copies, waits for them, and re-layouts  0.71 us (2%)
  between operations  0.68 us (1%)
    pallas_call x1, Pallas kernels, tail(): pl.pallas_call(functools.partial(tail_kernel, tp, sp, heads, hd), out_sha...  31.1 us
    pallas_call x1, Pallas kernels, attend(): pl.pallas_call(functools.partial(attend_kernel, heads=heads, all_heads=he...  14.1 us

profile of v4, /device:TPU:0, one launch (start us, length us, event | category | flops | bytes accessed | tf_op | source)
XLA Modules:
  0.0 46.6 jit_solution(10552781771632730126)
XLA Ops:
  0.6 0.0 copy-start
  0.6 0.0 copy-start.1
  0.7 14.1 %attend.1 = (f32[4,72,128]{2,1,0:T(8,128)S(1)}, bf16[64,512,128]{2,1,0:T(8,128)(2,1)}, bf16[64,512,128]{2,1,0:T(8,128)(2,1)}) custom-call(s32[64]{0:T(128)} %lens_hbm.1, bf16[64,2048]{1,0:T(8,128)(2,1)} %x_ref.1, f32[1,2048]{1,0:T(1,128)} %bitcast.13, bf16[24576,128]{1,0:T(8,128)(2,1)} %bitcast.11, bf16[64,512,128]{2,1,0:T(8,128)(2,1)} %bitcast.9, ...), custom_call_target="tpu_custom_call" | custom-call | tf_op jit(solution)/shard_map/attend/pallas_call | solution.py:323
  14.7 0.0 copy-done
  14.8 0.0 copy-done.1
  14.8 31.1 %tail.1 = bf16[64,2048]{1,0:T(8,128)(2,1)S(1)} custom-call(f32[4,72,128]{2,1,0:T(8,128)S(1)} %get-tuple-element.6.pay_ref, bf16[64,2048]{1,0:T(8,128)(2,1)S(1)} %copy-done, f32[1,2048]{1,0:T(1,128)S(1)} %bitcast.8, bf16[512,2048]{1,0:T(8,128)(2,1)} %bitcast.12, bf16[2048,2048]{1,0:T(8,128)(2,1)} %wu_hbm.1, bf16[2048,2048]{1,0:T(8,128)(2,1)} %wd_hbm.1), custom_call_target="tpu_custom_call" | custom-call | tf_op jit(solution)/shard_map/tail/pallas_call | solution.py:170
  45.9 0.7 %copy.14 = bf16[64,2048]{1,0:T(8,128)(2,1)} copy(bf16[64,2048]{1,0:T(8,128)(2,1)S(1)} %tail.1) | data formatting | bytes 524288
Async XLA Ops:
  0.6 14.1 %copy-start = (bf16[64,2048]{1,0:T(8,128)(2,1)S(1)}, bf16[64,2048]{1,0:T(8,128)(2,1)}, u32[]{:S(2)}) copy-start(bf16[64,2048]{1,0:T(8,128)(2,1)} %x_ref.1) | copy-start | bytes 786436
  0.6 14.1 %copy-start.1 = (f32[2048]{0:T(1024)S(1)}, f32[2048]{0:T(1024)}, u32[]{:S(2)}) copy-start(f32[2048]{0:T(1024)} %param.17) | copy-start | bytes 24580

commit v5 on v4

--- a/solution.py
+++ b/solution.py
@@ -22,8 +22,8 @@
     return 0.5 * x * (1.0 + lax.erf(x * (0.5 ** 0.5)))
 
 
-def tail_kernel(tp, sp, heads, hd, pay_ref, x_ref, gain_ref, wo_hbm, wu_hbm, wd_hbm, out_ref,
-                wo, wu, wd, got_pay, att, part, got_part, r_all, h_mid, hidden, down, got_down, x_all,
+def tail_kernel(tp, sp, heads, hd, stats_ref, p_ref, v_ref, x_ref, gain_ref, wo_hbm, wu_hbm, wd_hbm, out_ref,
+                wo, wu, wd, pay, got_pay, att, part, got_part, r_all, h_mid, hidden, down, got_down, x_all,
                 wo_sem, wu_sem, wd_sem, s1, r1, s2, r2, s3, r3, s4, r4, s5z, s5y, s5c, r5):
     my_tp = lax.axis_index("tp")
     my_sp = lax.axis_index("sp")
@@ -43,22 +43,35 @@
             copy.start()
             loads[name, j] = copy
 
-    pl.semaphore_wait(barrier, sp + tp - 2)
-
     sends = []
-    for off in range(1, sp):
-        peer = lax.rem(my_sp + off, sp)
-        copy = pltpu.make_async_remote_copy(
-            pay_ref.at[peer], got_pay.at[my_sp],
-            s1.at[off], r1.at[my_sp], device_id={"sp": peer}, device_id_type=MESH)
-        copy.start()
-        sends.append(copy)
+    side = lax.rem(my_sp + 2, sp)
+    twin = my_sp + 1 - 2 * lax.rem(my_sp, 2)
+    side_twin = lax.rem(twin + 2, sp)
+    order = [side, side_twin, twin, my_sp]
+    quad = 16 // heads
+    row_seq = lax.broadcasted_iota(jnp.int32, (16, hd), 0) // heads
+    for n, owner in enumerate(order):
+        for i in range(0, rows, quad):
+            first = owner * rows + i
+            weights = p_ref[pl.ds(pl.multiple_of(first * heads, 16), 16), :]
+            values = jnp.concatenate([v_ref[first + m] for m in range(quad)], axis=1)
+            out = jnp.dot(weights, values, preferred_element_type=jnp.float32)
+            pay[owner, i * heads:i * heads + 16, :] = sum(
+                jnp.where(row_seq == m, out[:, m * hd:(m + 1) * hd], 0.0) for m in range(quad))
+        pay[owner, rows * heads:, :] = stats_ref[owner]
+        if n == 0:
+            pl.semaphore_wait(barrier, sp + tp - 2)
+        if n < sp - 1:
+            copy = pltpu.make_async_remote_copy(pay.at[owner], got_pay.at[my_sp], s1.at[owner], r1.at[my_sp],
+                                                device_id={"sp": owner}, device_id_type=MESH)
+            copy.start()
+            sends.append(copy)
 
     def arrived(dst, sem):
         pltpu.make_async_copy(dst, dst, sem).wait()
 
     pairs = rows * heads
-    blocks = [pay_ref[my_sp]]
+    blocks = [pay[my_sp]]
     for off in range(1, sp):
         peer = lax.rem(my_sp + off, sp)
         arrived(got_pay.at[peer], r1.at[peer])
@@ -122,10 +135,6 @@
     for j in range(tp):
         loads["d", j].wait()
     total = reduce_scatter(hidden[...], wd, down, got_down, s4, r4)
-
-    side = lax.rem(my_sp + 2, sp)
-    twin = my_sp + 1 - 2 * lax.rem(my_sp, 2)
-    side_twin = lax.rem(twin + 2, sp)
 
     def pass_on(s, t, i, send_sem, to):
         send(x_all.at[s, t, i], x_all.at[s, t, i], send_sem, r5.at[s, t, i], to)
@@ -157,26 +166,27 @@
         copy.wait_send()
 
 
-def tail(tp, sp, heads, hd, pay, x_in, gain, w_out, w_up, w_down):
+def tail(tp, sp, heads, hd, stats, p, v, x_in, gain, w_out, w_up, w_down):
     batch, d = x_in.shape
     rows, cols = batch // sp, d // tp
     split = 1
     blocks = (tp, split, rows, cols // split)
     ff = w_up.shape[1]
     width = heads * hd
+    pay = (sp, rows * heads + 8, hd)
     vmem = pl.BlockSpec(memory_space=pltpu.VMEM)
     hbm = pl.BlockSpec(memory_space=pltpu.HBM)
     dma = pltpu.SemaphoreType.DMA
     return pl.pallas_call(
         functools.partial(tail_kernel, tp, sp, heads, hd),
         out_shape=jax.ShapeDtypeStruct((batch, d), jnp.bfloat16),
-        in_specs=[vmem, vmem, vmem, hbm, hbm, hbm],
+        in_specs=[vmem] * 5 + [hbm] * 3,
         out_specs=vmem,
         scratch_shapes=[
             pltpu.VMEM((tp, width, cols), jnp.bfloat16),
             pltpu.VMEM((tp, d, ff // tp), jnp.bfloat16),
             pltpu.VMEM((tp, ff, cols), jnp.bfloat16),
-            pltpu.VMEM(pay.shape, jnp.float32),
+            pltpu.VMEM(pay, jnp.float32), pltpu.VMEM(pay, jnp.float32),
             pltpu.VMEM((rows * heads, hd), jnp.float32),
             pltpu.VMEM(blocks, jnp.float32), pltpu.VMEM(blocks, jnp.float32), pltpu.VMEM(blocks, jnp.float32),
             pltpu.VMEM((rows, d), jnp.bfloat16),
@@ -188,11 +198,11 @@
         ],
         compiler_params=pltpu.CompilerParams(collective_id=0, has_side_effects=True, vmem_limit_bytes=24 * 2 ** 20),
         name="tail",
-    )(pay, x_in, gain[None, :], *(pltpu.with_memory_space_constraint(w, pltpu.HBM) for w in (w_out.reshape(width, d), w_up, w_down)))
-
-
-def attend_kernel(lens_hbm, x_hbm, gain_hbm, w_hbm, k_hbm, v_hbm, pay_ref, kn_hbm, vn_hbm,
-                  lens_ref, x_ref, gain_ref, wbuf, wide, normed, qkv, kbuf, vbuf, rep_k, rep_v, p_t,
+    )(stats, p, v, x_in, gain[None, :], *(pltpu.with_memory_space_constraint(w, pltpu.HBM) for w in (w_out.reshape(width, d), w_up, w_down)))
+
+
+def attend_kernel(lens_hbm, x_hbm, gain_hbm, w_hbm, k_hbm, v_hbm, stats_ref, p_t, vbuf, kn_hbm, vn_hbm,
+                  lens_ref, x_ref, gain_ref, wbuf, wide, normed, qkv, kbuf, rep_k, rep_v,
                   small_in, w_in, k_in, v_in, k_out, v_out, *, heads, all_heads, sp, chunks, ahead):
     batch, pairs, hd = kbuf.shape
     slots = pairs // heads
@@ -257,6 +267,11 @@
                 old = buf[b, span, :].astype(jnp.float32)
                 new = jnp.concatenate([rep[b // 2, b % 2]] * 2, axis=0)
                 buf[b, span, :] = jnp.where(row_slot == lax.rem(slot, 4), new, old).astype(buf.dtype)
+
+    def store_v(c):
+        loaded(pieces + chunks + c)
+        put_rows(vbuf, rep_v, c)
+        moves(vbuf, vn_hbm, v_out, c).start()
 
     q_t = qkv[0].T.astype(jnp.bfloat16)
     lane = lax.broadcasted_iota(jnp.int32, (1, 128), 1)
@@ -279,6 +294,8 @@
             part = jnp.dot(keys, query, preferred_element_type=jnp.float32)
             scores = part if scores is None else scores + part
             moves(kbuf, kn_hbm, k_out, c).start()
+            if c >= 1:
+                store_v(c - 1)
         length = jnp.zeros((1, 128), jnp.int32)
         for i in range(group):
             length = jnp.where(lane_seq == i, lens_ref[g * group + i], length)
@@ -290,22 +307,11 @@
         total = jnp.sum(p, axis=0, keepdims=True)
         stats = jnp.concatenate([top, total, jnp.zeros((6, 128), jnp.float32)], axis=0)
         for s in range(g * sp // (batch // group), (g + 1) * sp // (batch // group)):
-            pay_ref[s, batch // sp * heads:, :] = stats
+            stats_ref[s] = stats
         p_t[g * 128:(g + 1) * 128, :] = p.T.astype(jnp.bfloat16)
 
-    quad = 16 // heads
-    row_seq = lax.broadcasted_iota(jnp.int32, (16, hd), 0) // heads
-    for c in range(chunks):
-        loaded(pieces + chunks + c)
-        put_rows(vbuf, rep_v, c)
-        for b in range(c * per, (c + 1) * per, quad):
-            values = jnp.concatenate([vbuf[b + i] for i in range(quad)], axis=1)
-            out = jnp.dot(p_t[b * heads:b * heads + 16, :], values, preferred_element_type=jnp.float32)
-            out = sum(jnp.where(row_seq == i, out[:, i * hd:(i + 1) * hd], 0.0) for i in range(quad))
-            owner = b * sp // batch
-            at = (b - owner * (batch // sp)) * heads
-            pay_ref[owner, at:at + 16, :] = out
-        moves(vbuf, vn_hbm, v_out, c).start()
+    for c in range(chunks - 1, chunks):
+        store_v(c)
     for c in range(chunks):
         moves(kbuf, kn_hbm, k_out, c).wait()
         moves(vbuf, vn_hbm, v_out, c).wait()
@@ -314,31 +320,30 @@
 def attend(tp, sp, lens, x_in, gain, w_qkv, k_cache, v_cache):
     batch, slots, heads, hd = k_cache.shape
     d = x_in.shape[1]
-    chunks, pieces, ahead = 4, 4, 4
+    chunks, pieces, ahead = 4, 4, 5
     flat = (batch, slots * heads, hd)
     vmem = pl.BlockSpec(memory_space=pltpu.VMEM)
     hbm = pl.BlockSpec(memory_space=pltpu.HBM)
     dma = pltpu.SemaphoreType.DMA
     operands = (lens, x_in, gain[None, :], w_qkv.reshape(d * 3 * heads, hd), k_cache.reshape(flat), v_cache.reshape(flat))
-    pay, k_next, v_next = pl.pallas_call(
+    return pl.pallas_call(
         functools.partial(attend_kernel, heads=heads, all_heads=heads * tp, sp=sp, chunks=chunks, ahead=ahead),
-        out_shape=(jax.ShapeDtypeStruct((sp, batch // sp * heads + 8, hd), jnp.float32),
+        out_shape=(pltpu.VMEM((sp, 8, hd), jnp.float32), pltpu.VMEM((batch * heads, slots * heads), jnp.bfloat16),
+                   pltpu.VMEM(flat, v_cache.dtype),
                    jax.ShapeDtypeStruct(flat, k_cache.dtype), jax.ShapeDtypeStruct(flat, v_cache.dtype)),
         in_specs=[hbm] * len(operands),
-        out_specs=(vmem, hbm, hbm),
+        out_specs=(vmem, vmem, vmem, hbm, hbm),
         scratch_shapes=[
             pltpu.SMEM(lens.shape, lens.dtype), pltpu.VMEM(x_in.shape, x_in.dtype), pltpu.VMEM((1, d), gain.dtype),
             pltpu.VMEM((d * 3 * heads, hd), jnp.bfloat16), pltpu.VMEM((d // pieces * 3 * heads, hd), jnp.float32),
             pltpu.VMEM((batch, d), jnp.bfloat16), pltpu.VMEM((3, batch * heads, hd), jnp.float32),
-            pltpu.VMEM(flat, k_cache.dtype), pltpu.VMEM(flat, v_cache.dtype),
+            pltpu.VMEM(flat, k_cache.dtype),
             pltpu.VMEM((batch // 2, 2, 8, hd), jnp.float32), pltpu.VMEM((batch // 2, 2, 8, hd), jnp.float32),
-            pltpu.VMEM((batch * heads, slots * heads), jnp.bfloat16),
             dma((3,)), dma((pieces,)), dma((chunks,)), dma((chunks,)), dma((chunks,)), dma((chunks,)),
         ],
         compiler_params=pltpu.CompilerParams(vmem_limit_bytes=36 * 2 ** 20),
         name="attend",
     )(*(pltpu.with_memory_space_constraint(a, pltpu.HBM) for a in operands))
-    return pay, k_next.reshape(k_cache.shape), v_next.reshape(v_cache.shape)
 
 
 def solution(mesh):
@@ -348,9 +353,9 @@
     def local_layer(x_in, seq_lens, k_cache, v_cache, ln1_gain, w_qkv, w_out, ln2_gain, w_up, w_down):
         local_heads = k_cache.shape[2]
         head_dim = k_cache.shape[3]
-        pay, k_next, v_next = attend(tp_size, sp_size, seq_lens, x_in, ln1_gain, w_qkv, k_cache, v_cache)
-        x_out = tail(tp_size, sp_size, local_heads, head_dim, pay, x_in, ln2_gain, w_out, w_up, w_down)
-        return x_out, k_next, v_next
+        stats, p, v, k_next, v_next = attend(tp_size, sp_size, seq_lens, x_in, ln1_gain, w_qkv, k_cache, v_cache)
+        x_out = tail(tp_size, sp_size, local_heads, head_dim, stats, p, v, x_in, ln2_gain, w_out, w_up, w_down)
+        return x_out, k_next.reshape(k_cache.shape), v_next.reshape(v_cache.shape)
 
     cache_spec = P("dp", "sp", "tp", None)
     in_specs = (P("dp", None), P("dp"), cache_spec, cache_spec, P(None), P(None, None, "tp", None), P("tp", None, None), P(None), P(None, "tp"), P("tp", None))

time: 46.7 us -> 47 us (level)
    pallas_call x1, Pallas kernels: 31.1 us -> 32.2 us  [tail(): pl.pallas_call(functools.partial(tail_kernel, tp, sp, heads, hd), out_sha...]
    pallas_call x1, Pallas kernels: 14.1 us -> 13.3 us  [attend(): pl.pallas_call(functools.partial(attend_kernel, heads=heads, all_heads=he...]
where the time goes in v5:
time: 47 us; the launch traced here: 46.8 us
  Pallas kernels  45.4 us (97%)
  local copies, waits for them, and re-layouts  0.71 us (2%)
  between operations  0.68 us (1%)
    pallas_call x1, Pallas kernels, tail(): pl.pallas_call(functools.partial(tail_kernel, tp, sp, heads, hd), out_sha...  32.2 us
    pallas_call x1, Pallas kernels, attend(): pl.pallas_call(functools.partial(attend_kernel, heads=heads, all_heads=he...  13.3 us

profile of v5, /device:TPU:0, one launch (start us, length us, event | category | flops | bytes accessed | tf_op | source)
XLA Modules:
  0.0 46.8 jit_solution(15298639909654175889)
XLA Ops:
  0.6 0.0 copy-start
  0.6 0.0 copy-start.1
  0.7 13.3 %attend.1 = (f32[4,8,128]{2,1,0:T(8,128)S(1)}, bf16[256,512]{1,0:T(8,128)(2,1)S(1)}, bf16[64,512,128]{2,1,0:T(8,128)(2,1)S(1)}, bf16[64,512,128]{2,1,0:T(8,128)(2,1)}, bf16[64,512,128]{2,1,0:T(8,128)(2,1)}) custom-call(s32[64]{0:T(128)} %lens_hbm.1, bf16[64,2048]{1,0:T(8,128)(2,1)} %x_ref.1, f32[1,2048]{1,0:T(1,128)} %bitcast.13, ...), custom_call_target="tpu_custom_call" | custom-call | tf_op jit(solution)/shard_map/attend/pallas_call | solution.py:329
  13.9 0.0 copy-done
  13.9 0.0 copy-done.1
  13.9 32.2 %tail.1 = bf16[64,2048]{1,0:T(8,128)(2,1)S(1)} custom-call(f32[4,8,128]{2,1,0:T(8,128)S(1)} %get-tuple-element.8.stats_ref, bf16[256,512]{1,0:T(8,128)(2,1)S(1)} %get-tuple-element.9.p_ref, bf16[64,512,128]{2,1,0:T(8,128)(2,1)S(1)} %get-tuple-element.10.v_ref, bf16[64,2048]{1,0:T(8,128)(2,1)S(1)} %copy-done, f32[1,2048]{1,0:T(1,128)S(1)} %bitcast.8, ...), custom_call_target="tpu_custom_call" | custom-call | tf_op jit(solution)/shard_map/tail/pallas_call | solution.py:180
  46.1 0.7 %copy.14 = bf16[64,2048]{1,0:T(8,128)(2,1)} copy(bf16[64,2048]{1,0:T(8,128)(2,1)S(1)} %tail.1) | data formatting | bytes 524288
Async XLA Ops:
  0.6 13.3 %copy-start = (bf16[64,2048]{1,0:T(8,128)(2,1)S(1)}, bf16[64,2048]{1,0:T(8,128)(2,1)}, u32[]{:S(2)}) copy-start(bf16[64,2048]{1,0:T(8,128)(2,1)} %x_ref.1) | copy-start | bytes 786436
  0.6 13.3 %copy-start.1 = (f32[2048]{0:T(1024)S(1)}, f32[2048]{0:T(1024)}, u32[]{:S(2)}) copy-start(f32[2048]{0:T(1024)} %param.17) | copy-start | bytes 24580

commit v6 on v4

--- a/solution.py
+++ b/solution.py
@@ -45,9 +45,11 @@
 
     pl.semaphore_wait(barrier, sp + tp - 2)
 
+    side = lax.rem(my_sp + 2, sp)
+    twin = my_sp + 1 - 2 * lax.rem(my_sp, 2)
+    side_twin = lax.rem(twin + 2, sp)
     sends = []
-    for off in range(1, sp):
-        peer = lax.rem(my_sp + off, sp)
+    for off, peer in enumerate((side, side_twin, twin)):
         copy = pltpu.make_async_remote_copy(
             pay_ref.at[peer], got_pay.at[my_sp],
             s1.at[off], r1.at[my_sp], device_id={"sp": peer}, device_id_type=MESH)
@@ -123,9 +125,6 @@
         loads["d", j].wait()
     total = reduce_scatter(hidden[...], wd, down, got_down, s4, r4)
 
-    side = lax.rem(my_sp + 2, sp)
-    twin = my_sp + 1 - 2 * lax.rem(my_sp, 2)
-    side_twin = lax.rem(twin + 2, sp)
 
     def pass_on(s, t, i, send_sem, to):
         send(x_all.at[s, t, i], x_all.at[s, t, i], send_sem, r5.at[s, t, i], to)
@@ -258,6 +257,11 @@
                 new = jnp.concatenate([rep[b // 2, b % 2]] * 2, axis=0)
                 buf[b, span, :] = jnp.where(row_slot == lax.rem(slot, 4), new, old).astype(buf.dtype)
 
+    def store_v(c):
+        loaded(pieces + chunks + c)
+        put_rows(vbuf, rep_v, c)
+        moves(vbuf, vn_hbm, v_out, c).start()
+
     q_t = qkv[0].T.astype(jnp.bfloat16)
     lane = lax.broadcasted_iota(jnp.int32, (1, 128), 1)
     lane_seq, lane_head = lane // heads, lax.rem(lane, heads)
@@ -279,6 +283,8 @@
             part = jnp.dot(keys, query, preferred_element_type=jnp.float32)
             scores = part if scores is None else scores + part
             moves(kbuf, kn_hbm, k_out, c).start()
+            if c > 0:
+                store_v(c - 1)
         length = jnp.zeros((1, 128), jnp.int32)
         for i in range(group):
             length = jnp.where(lane_seq == i, lens_ref[g * group + i], length)
@@ -296,8 +302,8 @@
     quad = 16 // heads
     row_seq = lax.broadcasted_iota(jnp.int32, (16, hd), 0) // heads
     for c in range(chunks):
-        loaded(pieces + chunks + c)
-        put_rows(vbuf, rep_v, c)
+        if c == 0:
+            store_v(chunks - 1)
         for b in range(c * per, (c + 1) * per, quad):
             values = jnp.concatenate([vbuf[b + i] for i in range(quad)], axis=1)
             out = jnp.dot(p_t[b * heads:b * heads + 16, :], values, preferred_element_type=jnp.float32)
@@ -305,7 +311,6 @@
             owner = b * sp // batch
             at = (b - owner * (batch // sp)) * heads
             pay_ref[owner, at:at + 16, :] = out
-        moves(vbuf, vn_hbm, v_out, c).start()
     for c in range(chunks):
         moves(kbuf, kn_hbm, k_out, c).wait()
         moves(vbuf, vn_hbm, v_out, c).wait()
@@ -314,7 +319,7 @@
 def attend(tp, sp, lens, x_in, gain, w_qkv, k_cache, v_cache):
     batch, slots, heads, hd = k_cache.shape
     d = x_in.shape[1]
-    chunks, pieces, ahead = 4, 4, 4
+    chunks, pieces, ahead = 4, 4, 6
     flat = (batch, slots * heads, hd)
     vmem = pl.BlockSpec(memory_space=pltpu.VMEM)
     hbm = pl.BlockSpec(memory_space=pltpu.HBM)

time: 46.7 us -> 46 us (0.985)
  Pallas kernels: 45.2 us -> 44.1 us
    pallas_call x1, Pallas kernels: 14.1 us -> 13.3 us  [attend(): pl.pallas_call(functools.partial(attend_kernel, heads=heads, all_heads=he...]
where the time goes in v6:
time: 46 us; the launch traced here: 45.5 us
  Pallas kernels  44.1 us (96%)
  local copies, waits for them, and re-layouts  0.71 us (2%)
  between operations  0.68 us (1%)
    pallas_call x1, Pallas kernels, tail(): pl.pallas_call(functools.partial(tail_kernel, tp, sp, heads, hd), out_sha...  30.8 us
    pallas_call x1, Pallas kernels, attend(): pl.pallas_call(functools.partial(attend_kernel, heads=heads, all_heads=he...  13.3 us

profile of v6, /device:TPU:0, one launch (start us, length us, event | category | flops | bytes accessed | tf_op | source)
XLA Modules:
  0.0 45.5 jit_solution(9866251661116501395)
XLA Ops:
  0.6 0.0 copy-start
  0.6 0.0 copy-start.1
  0.7 13.3 %attend.1 = (f32[4,72,128]{2,1,0:T(8,128)S(1)}, bf16[64,512,128]{2,1,0:T(8,128)(2,1)}, bf16[64,512,128]{2,1,0:T(8,128)(2,1)}) custom-call(s32[64]{0:T(128)} %lens_hbm.1, bf16[64,2048]{1,0:T(8,128)(2,1)} %x_ref.1, f32[1,2048]{1,0:T(1,128)} %bitcast.13, bf16[24576,128]{1,0:T(8,128)(2,1)} %bitcast.11, bf16[64,512,128]{2,1,0:T(8,128)(2,1)} %bitcast.9, ...), custom_call_target="tpu_custom_call" | custom-call | tf_op jit(solution)/shard_map/attend/pallas_call | solution.py:328
  13.9 0.0 copy-done
  13.9 0.0 copy-done.1
  14.0 30.8 %tail.1 = bf16[64,2048]{1,0:T(8,128)(2,1)S(1)} custom-call(f32[4,72,128]{2,1,0:T(8,128)S(1)} %get-tuple-element.6.pay_ref, bf16[64,2048]{1,0:T(8,128)(2,1)S(1)} %copy-done, f32[1,2048]{1,0:T(1,128)S(1)} %bitcast.8, bf16[512,2048]{1,0:T(8,128)(2,1)} %bitcast.12, bf16[2048,2048]{1,0:T(8,128)(2,1)} %wu_hbm.1, bf16[2048,2048]{1,0:T(8,128)(2,1)} %wd_hbm.1), custom_call_target="tpu_custom_call" | custom-call | tf_op jit(solution)/shard_map/tail/pallas_call | solution.py:169
  44.8 0.7 %copy.14 = bf16[64,2048]{1,0:T(8,128)(2,1)} copy(bf16[64,2048]{1,0:T(8,128)(2,1)S(1)} %tail.1) | data formatting | bytes 524288
Async XLA Ops:
  0.6 13.3 %copy-start = (bf16[64,2048]{1,0:T(8,128)(2,1)S(1)}, bf16[64,2048]{1,0:T(8,128)(2,1)}, u32[]{:S(2)}) copy-start(bf16[64,2048]{1,0:T(8,128)(2,1)} %x_ref.1) | copy-start | bytes 786436
  0.6 13.3 %copy-start.1 = (f32[2048]{0:T(1024)S(1)}, f32[2048]{0:T(1024)}, u32[]{:S(2)}) copy-start(f32[2048]{0:T(1024)} %param.17) | copy-start | bytes 24580

commit v7 on v6

--- a/solution.py
+++ b/solution.py
@@ -49,7 +49,8 @@
     twin = my_sp + 1 - 2 * lax.rem(my_sp, 2)
     side_twin = lax.rem(twin + 2, sp)
     sends = []
-    for off, peer in enumerate((side, side_twin, twin)):
+    for off in range(1, sp):
+        peer = lax.rem(my_sp + off, sp)
         copy = pltpu.make_async_remote_copy(
             pay_ref.at[peer], got_pay.at[my_sp],
             s1.at[off], r1.at[my_sp], device_id={"sp": peer}, device_id_type=MESH)

time: 46 us -> 46 us (level)
  no operation moved by 1% of the time
where the time goes in v7:
time: 46 us; the launch traced here: 45.8 us
  Pallas kernels  44.4 us (97%)
  local copies, waits for them, and re-layouts  0.71 us (2%)
  between operations  0.68 us (1%)
    pallas_call x1, Pallas kernels, tail(): pl.pallas_call(functools.partial(tail_kernel, tp, sp, heads, hd), out_sha...  31.1 us
    pallas_call x1, Pallas kernels, attend(): pl.pallas_call(functools.partial(attend_kernel, heads=heads, all_heads=he...  13.3 us

profile of v7, /device:TPU:0, one launch (start us, length us, event | category | flops | bytes accessed | tf_op | source)
XLA Modules:
  0.0 45.8 jit_solution(13472638102044119226)
XLA Ops:
  0.6 0.0 copy-start
  0.6 0.0 copy-start.1
  0.7 13.3 %attend.1 = (f32[4,72,128]{2,1,0:T(8,128)S(1)}, bf16[64,512,128]{2,1,0:T(8,128)(2,1)}, bf16[64,512,128]{2,1,0:T(8,128)(2,1)}) custom-call(s32[64]{0:T(128)} %lens_hbm.1, bf16[64,2048]{1,0:T(8,128)(2,1)} %x_ref.1, f32[1,2048]{1,0:T(1,128)} %bitcast.13, bf16[24576,128]{1,0:T(8,128)(2,1)} %bitcast.11, bf16[64,512,128]{2,1,0:T(8,128)(2,1)} %bitcast.9, ...), custom_call_target="tpu_custom_call" | custom-call | tf_op jit(solution)/shard_map/attend/pallas_call | solution.py:329
  13.9 0.0 copy-done
  13.9 0.0 copy-done.1
  13.9 31.1 %tail.1 = bf16[64,2048]{1,0:T(8,128)(2,1)S(1)} custom-call(f32[4,72,128]{2,1,0:T(8,128)S(1)} %get-tuple-element.6.pay_ref, bf16[64,2048]{1,0:T(8,128)(2,1)S(1)} %copy-done, f32[1,2048]{1,0:T(1,128)S(1)} %bitcast.8, bf16[512,2048]{1,0:T(8,128)(2,1)} %bitcast.12, bf16[2048,2048]{1,0:T(8,128)(2,1)} %wu_hbm.1, bf16[2048,2048]{1,0:T(8,128)(2,1)} %wd_hbm.1), custom_call_target="tpu_custom_call" | custom-call | tf_op jit(solution)/shard_map/tail/pallas_call | solution.py:170
  45.0 0.7 %copy.14 = bf16[64,2048]{1,0:T(8,128)(2,1)} copy(bf16[64,2048]{1,0:T(8,128)(2,1)S(1)} %tail.1) | data formatting | bytes 524288
Async XLA Ops:
  0.6 13.3 %copy-start = (bf16[64,2048]{1,0:T(8,128)(2,1)S(1)}, bf16[64,2048]{1,0:T(8,128)(2,1)}, u32[]{:S(2)}) copy-start(bf16[64,2048]{1,0:T(8,128)(2,1)} %x_ref.1) | copy-start | bytes 786436
  0.6 13.3 %copy-start.1 = (f32[2048]{0:T(1024)S(1)}, f32[2048]{0:T(1024)}, u32[]{:S(2)}) copy-start(f32[2048]{0:T(1024)} %param.17) | copy-start | bytes 24580
